TPU v7x, 32 devices: a whole 2x2x4 slice. The times are simulated.
32 devices in a mesh: groups: 2 (over y), section: 4 (over z), seq: 4 (over x, core).
Axes of the slice: x: 2, y: 2, z: 4, core: 2. Of those that a mesh axis runs over, the one named last changes fastest.
Arguments:
- tokens: bfloat16 [8, 256, 1440], P('groups', 'seq'), parts along dimension 0, may hold values from -6 to 6
- block_order: int32 [8], P('groups'), parts along dimension 0, may hold values from 0 to 3, each once
- prompt_lengths: int32 [8], P('groups'), parts along dimension 0, may hold values from 1 to 256, 576 in all
- norm_gain: float32 [4, 1440], P('section'), may hold values from 0.1 to 1.9
- w_query: bfloat16 [4, 1440, 2048], P('section', None, 'seq'), may hold values from -4 to 4
- w_key_value: bfloat16 [4, 1440, 512], P('section'), may hold values from -4 to 4
- w_out: bfloat16 [4, 2048, 1440], P('section', 'seq'), may hold values from -0.125 to 0.125
- sink_logits: float32 [4, 32], P('section'), may hold values from 0 to 4
Outputs:
- hidden_states: bfloat16 [4, 8, 256, 1440], P('section', 'groups', 'seq'), parts along dimension 1
- layer_cache: bfloat16 [4, 8, 256, 512], P('section', 'groups', 'seq'), parts along dimension 1
There are 2 independent parts, one for each index of `groups`. A program takes and returns all parts, laid end to end along the dimension named above; an argument that names none is the same for every part. Nothing has to cross between parts.
Inputs may be any that keep to these rules, and one draw needn't show every extreme that they name: `block_order`: each of 0 to 3 exactly once. `prompt_lengths`: the longest prompt is full.
All inputs are finite; a program needn't handle non-finite values.
Results may differ from a plain program's by a relative error of at most 0.024.
Values may be sent and summed in bfloat16 or wider, within the bound.
A program may use at most 128 MiB of HBM per device.

v0:
```python
import functools
import math

import jax
import jax.numpy as jnp
from jax import lax
from jax.experimental import pallas as pl
from jax.experimental.pallas import tpu as pltpu
from jax.sharding import PartitionSpec as P

HEAD_DIM = 64
WIN = 128
LANES = 128


THETA = 150000.0
EPSILON = 1e-05
MESH = pl.DeviceIdType.MESH
F32 = jnp.float32
BF16 = jnp.bfloat16
QUERY_CUTS = 3
OUT_CUTS = 3
HOP_CUTS = 3


def rotary(positions, head_size):
    half = head_size // 2
    freq = jnp.exp(jnp.arange(half, dtype=F32) * (-2.0 * math.log(THETA) / head_size))
    angles = positions.astype(F32)[:, None] * freq[None, :]
    return jnp.cos(angles), jnp.sin(angles)


def kernel(
    shape,
    order_ref, length_ref, sink_ref,
    tokens_ref, gain_ref, cos_ref, sin_ref, pair_ref, query_hbm, out_hbm,
    hidden_ref, cache_ref,
    query_w, out_w, arrive, window, hbuf, normed_ref, qbuf, cbuf,
    local_sem, x_send, x_recv, y_send, y_recv, d_send, d_recv, own_send, own_recv,
    w_send, w_recv, z_send, z_recv,
):
    groups, sections, seq = shape
    chips = seq // 2
    g = lax.axis_index("groups")
    sec = lax.axis_index("section")
    q = lax.axis_index("seq")
    chip, core = q // 2, q % 2
    partner = chip * 2 + (1 - core)
    micro, rows, width = tokens_ref.shape
    shard = query_w.shape[2]
    heads_width = seq * shard
    kv_width = pair_ref.shape[1] // 2
    kv_heads = kv_width // HEAD_DIM
    group = heads_width // kv_width
    keep = min(WIN, rows)
    depth = WIN // keep

    mine = [
        pltpu.make_async_copy(query_hbm, query_w.at[q], local_sem.at[0]),
        pltpu.make_async_copy(
            out_hbm, out_w.at[:, pl.ds(pl.multiple_of(q * shard, shard), shard)], local_sem.at[1]
        ),
    ]
    for copy in mine:
        copy.start()

    barrier = pltpu.get_barrier_semaphore()
    greeted = 0
    for d in range(1, seq):
        pl.semaphore_signal(barrier, 1, device_id={"seq": (q + d) % seq}, device_id_type=MESH)
        greeted += 1
    for e in range(1, groups):
        pl.semaphore_signal(barrier, 1, device_id={"groups": (g + e) % groups}, device_id_type=MESH)
        greeted += 1
    for s in sorted({1 % sections, (sections - 1) % sections} - {0}):
        pl.semaphore_signal(barrier, 1, device_id={"section": (sec + s) % sections}, device_id_type=MESH)
        greeted += 1
    for off in range(1, depth + 1):

        @pl.when(q < off)
        def _():
            window[:, off - 1] = jnp.zeros((micro, keep, 2 * kv_width), BF16)

    pl.semaphore_wait(barrier, greeted)

    cuts = (QUERY_CUTS, OUT_CUTS)
    lengths = (width // groups // QUERY_CUTS, width // groups // OUT_CUTS)

    def piece(kind, owner, part, k):
        size = lengths[kind]
        first = (part * cuts[kind] + k) * size
        if kind == 0:
            return query_w.at[owner, pl.ds(pl.multiple_of(first, 16), size)]
        return out_w.at[
            pl.ds(pl.multiple_of(first, 16), size), pl.ds(pl.multiple_of(owner * shard, shard), shard)
        ]

    def whole(kind, owner):
        if kind == 0:
            return query_w.at[owner]
        return out_w.at[:, pl.ds(pl.multiple_of(owner * shard, shard), shard)]

    def remote(ref, send, recv, target):
        return pltpu.make_async_remote_copy(
            src_ref=ref, dst_ref=ref, send_sem=send, recv_sem=recv,
            device_id=target, device_id_type=MESH,
        )

    def x_copy(kind, d, k, owner):
        return remote(
            piece(kind, owner, g, k), x_send.at[kind, d, k], x_recv.at[kind, d, k],
            {"seq": ((chip + d) % chips) * 2 + core},
        )

    def y_copy(kind, d, k, e, owner, part):
        return remote(
            piece(kind, owner, part, k), y_send.at[kind, d, k, e], y_recv.at[kind, d, k, e],
            {"groups": (g + e) % groups},
        )

    def d_copy(kind, d, k, e, owner):
        return remote(
            piece(kind, owner, (g - e + groups) % groups, k), d_send.at[kind, d, k, e],
            d_recv.at[kind, d, k, e], {"seq": partner},
        )

    def own_copy(kind, owner):
        return remote(whole(kind, owner), own_send.at[kind], own_recv.at[kind], {"seq": partner})

    plan = [(kind, k, d) for kind in range(2) for k in range(cuts[kind]) for d in range(1, chips)]
    for kind in range(2):
        mine[kind].wait()
        for k in range(cuts[kind]):
            for d in range(1, chips):
                x_copy(kind, d, k, q).start()
        own_copy(kind, q).start()

    lane = lax.broadcasted_iota(jnp.int32, (rows, LANES), 1)
    first_half = (lane % HEAD_DIM) < (HEAD_DIM // 2)
    low = lane < HEAD_DIM
    cosine = cos_ref[...]
    sine = sin_ref[...]
    half = HEAD_DIM // 2

    def rotate(tile):
        swapped = jnp.where(
            first_half, pltpu.roll(tile, LANES - half, 1), pltpu.roll(tile, half, 1)
        )
        return tile * cosine + swapped * sine

    step = -(-width // (HOP_CUTS * LANES)) * LANES
    edges = [(c * step, min(step, width - c * step)) for c in range(HOP_CUTS)]

    def z_copy(t, c):
        columns = pl.ds(*edges[c])
        return pltpu.make_async_remote_copy(
            src_ref=hidden_ref.at[t, :, columns], dst_ref=arrive.at[t, :, columns],
            send_sem=z_send.at[t, c], recv_sem=z_recv.at[t, c], device_id={"section": (sec + 1) % sections}, device_id_type=MESH,
        )

    def w_copy(t, off, side):
        columns = pl.ds(side * kv_width, kv_width)
        return pltpu.make_async_remote_copy(
            src_ref=cache_ref.at[t, pl.ds(rows - keep, keep), columns],
            dst_ref=window.at[t, off - 1, :, columns],
            send_sem=w_send.at[t, off - 1, side], recv_sem=w_recv.at[t, off - 1, side],
            device_id={"seq": (q + off) % seq}, device_id_type=MESH,
        )

    def enter(t):
        block = order_ref[t]

        @pl.when(sec == 0)
        def _():
            hbuf[t] = tokens_ref[block]

        @pl.when(sec > 0)
        def _():
            for c in range(HOP_CUTS):
                z_copy(t, c).wait_recv()
            hbuf[t] = arrive[t]

        widened = hbuf[t].astype(F32)
        scale = lax.rsqrt(jnp.mean(widened * widened, -1, keepdims=True) + EPSILON)
        normed_ref[t] = (widened * scale * gain_ref[...]).astype(BF16)
        keys = jnp.dot(normed_ref[t], pair_ref[:, :kv_width], preferred_element_type=F32)
        for p in range(kv_width // LANES):
            tile = slice(p * LANES, (p + 1) * LANES)
            cache_ref[t, :, tile] = rotate(keys[:, tile]).astype(BF16)
        for off in range(1, depth + 1):

            @pl.when(q + off < seq)
            def _():
                w_copy(t, off, 0).start()

        values = jnp.dot(normed_ref[t], pair_ref[:, kv_width:], preferred_element_type=F32)
        cache_ref[t, :, kv_width:] = values.astype(BF16)
        for off in range(1, depth + 1):

            @pl.when(q + off < seq)
            def _():
                w_copy(t, off, 1).start()

    def attend(t, heads):
        length = length_ref[order_ref[t]]
        normed = normed_ref[t]

        def ask(s):
            queries = jnp.dot(normed, query_w[s], preferred_element_type=F32)
            for p in range(shard // LANES):
                rotated = rotate(queries[:, p * LANES:(p + 1) * LANES]) * 0.125
                qbuf[:, s * shard + p * LANES:s * shard + (p + 1) * LANES] = rotated.astype(BF16)

        per_head = seq // kv_heads
        for s in range(heads[0] * per_head, (heads[-1] + 1) * per_head):
            ask(s)

        if heads[0] == 0:
            for off in range(1, depth + 1):

                @pl.when(q >= off)
                def _():
                    w_copy(t, off, 0).wait_recv()
                    w_copy(t, off, 1).wait_recv()

        span = WIN + rows
        row = lax.broadcasted_iota(jnp.int32, (rows, span), 0)
        col = lax.broadcasted_iota(jnp.int32, (rows, span), 1) - WIN
        column = col + q * rows
        allowed = (col <= row) & (row - col < WIN) & (column >= 0)
        allowed = allowed & ((column < length) | (col == row))
        bias = jnp.where(allowed, F32(0.0), F32(-1e30))
        tiles = group // 2

        def span_of(first):
            at = slice(first, first + HEAD_DIM)
            parts = [window[t, off - 1, :, at] for off in range(depth, 0, -1)]
            return jnp.concatenate(parts + [cache_ref[t, :, at]], 0)

        def score(h):
            head = span_of(h * HEAD_DIM)
            stack = []
            for p in range(tiles):
                at = (h * tiles + p) * LANES
                pair = qbuf[:, at:at + LANES]
                zero = jnp.zeros_like(pair)
                stack += [jnp.where(low, pair, zero), jnp.where(low, zero, pair)]
            return lax.dot_general(
                jnp.concatenate(stack, 0), jnp.concatenate([head, head], 1),
                (((1,), (1,)), ((), ())), preferred_element_type=F32,
            )

        def mix(h, scores):
            head = span_of(kv_width + h * HEAD_DIM)
            values = jnp.concatenate([head, head, jnp.ones((span, LANES), BF16)], 1)
            expos, rest = [], []
            for j in range(group):
                sink = sink_ref[h * group + j]
                masked = scores[j * rows:(j + 1) * rows] + bias
                top = jnp.maximum(jnp.max(masked, -1, keepdims=True), sink)
                expos.append(jnp.exp(masked - top).astype(BF16))
                rest.append(jnp.exp(sink - top))
            summed = jnp.dot(jnp.concatenate(expos, 0), values, preferred_element_type=F32)
            for p in range(tiles):
                at = (h * tiles + p) * LANES
                sides = []
                for j in (2 * p, 2 * p + 1):
                    some = summed[j * rows:(j + 1) * rows]
                    sides.append((some[:, :LANES], some[:, LANES:] + rest[j]))
                context = jnp.where(low, sides[0][0], sides[1][0])
                context = context / jnp.where(low, sides[0][1], sides[1][1])
                cbuf[:, at:at + LANES] = context.astype(BF16)

        scores = score(heads[0])
        for h in heads:
            following = score(h + 1) if h + 1 in heads else None
            mix(h, scores)
            scores = following

    @pl.when(sec == 0)
    def _():
        @pl.loop(0, micro)
        def _(t):
            enter(t)

    def source(d, which):
        return ((chip - d + chips) % chips) * 2 + which

    def relay_y(kind, k, d):
        for e in range(1, groups):
            y_copy(kind, d, k, e, source(d, core), (g - e + groups) % groups).wait_recv()
            d_copy(kind, d, k, e, source(d, core)).start()

    previous = None
    for kind, k, d in plan:
        x_copy(kind, d, k, source(d, core)).wait_recv()
        for e in range(1, groups):
            y_copy(kind, d, k, e, source(d, core), g).start()
        d_copy(kind, d, k, 0, source(d, core)).start()
        if previous is not None:
            relay_y(*previous)
        previous = (kind, k, d)
        if kind == 1 and d == 1 and k == 1:
            own_copy(0, partner).wait_recv()
            for one in plan:
                if one[0] == 0:
                    for e in range(groups):
                        d_copy(*one[:1], one[2], one[1], e, source(one[2], 1 - core)).wait_recv()
        if kind == 1 and d == 1 and k >= 1:
            share = kv_heads // 2

            @pl.when(sec == 0)
            def _():
                attend(0, tuple(range((k - 1) * share, k * share)))

    if previous is not None:
        relay_y(*previous)
    own_copy(1, partner).wait_recv()
    for kind, k, d in plan:
        for e in range(groups if kind else 0):
            d_copy(kind, d, k, e, source(d, 1 - core)).wait_recv()

    def slot(t, carry):
        @pl.when(sec > 0)
        def _():
            enter(t)

        @pl.when((sec > 0) | (t > 0))
        def _():
            attend(t, tuple(range(kv_heads)))

        for c, (first, size) in enumerate(edges):
            output = lax.dot_general(
                cbuf[...], out_w[first:first + size], (((1,), (1,)), ((), ())),
                preferred_element_type=F32,
            )
            columns = slice(first, first + size)
            hidden_ref[t, :, columns] = (hbuf[t, :, columns].astype(F32) + output).astype(BF16)

            @pl.when(sec + 1 < sections)
            def _():
                z_copy(t, c).start()

        return carry

    lax.fori_loop(0, micro, slot, 0)

    for kind, k, d in plan:
        x_copy(kind, d, k, q).wait_send()
        for e in range(1, groups):
            y_copy(kind, d, k, e, source(d, core), g).wait_send()
        for e in range(groups):
            d_copy(kind, d, k, e, source(d, core)).wait_send()
    for kind in range(2):
        own_copy(kind, q).wait_send()
    for t in range(micro):
        for off in range(1, depth + 1):

            @pl.when(q + off < seq)
            def _():
                w_copy(t, off, 0).wait_send()
                w_copy(t, off, 1).wait_send()

        @pl.when(sec + 1 < sections)
        def _():
            for c in range(HOP_CUTS):
                z_copy(t, c).wait_send()


def per_device(
    shape,
    tokens, block_order, prompt_lengths, norm_gain, w_query, w_key_value, w_out, sink_logits
):
    groups, sections, seq = shape
    micro, rows, width = tokens.shape
    shard = w_query.shape[2]
    pair_width = w_key_value.shape[2]
    chips = seq // 2
    keep = min(WIN, rows)
    depth = WIN // keep
    positions = lax.axis_index("seq") * rows + jnp.arange(rows, dtype=jnp.int32)
    cosine, sine = rotary(positions, HEAD_DIM)
    repeat = LANES // HEAD_DIM
    cosine = jnp.tile(jnp.concatenate([cosine, cosine], 1), (1, repeat))
    sine = jnp.tile(jnp.concatenate([-sine, sine], 1), (1, repeat))
    most = max(QUERY_CUTS, OUT_CUTS)
    dma = pltpu.SemaphoreType.DMA
    vmem = pl.BlockSpec(memory_space=pltpu.VMEM)
    smem = pl.BlockSpec(memory_space=pltpu.SMEM)
    hbm = pl.BlockSpec(memory_space=pl.ANY)
    hidden, cache = pl.pallas_call(
        functools.partial(kernel, shape),
        out_shape=(
            jax.ShapeDtypeStruct((micro, rows, width), BF16),
            jax.ShapeDtypeStruct((micro, rows, pair_width), BF16),
        ),
        in_specs=[smem] * 3 + [vmem] * 5 + [hbm] * 2,
        out_specs=(vmem, vmem),
        scratch_shapes=[
            pltpu.VMEM((seq, width, shard), BF16),
            pltpu.VMEM((width, seq * shard), BF16),
            pltpu.VMEM((micro, rows, width), BF16),
            pltpu.VMEM((micro, depth, keep, pair_width), BF16),
            pltpu.VMEM((micro, rows, width), BF16),
            pltpu.VMEM((micro, rows, width), BF16),
            pltpu.VMEM((rows, seq * shard), BF16),
            pltpu.VMEM((rows, seq * shard), BF16),
            dma((2,)),
            dma((2, chips, most)),
            dma((2, chips, most)),
            dma((2, chips, most, groups)),
            dma((2, chips, most, groups)),
            dma((2, chips, most, groups)),
            dma((2, chips, most, groups)),
            dma((2,)),
            dma((2,)),
            dma((micro, depth, 2)),
            dma((micro, depth, 2)),
            dma((micro, HOP_CUTS)),
            dma((micro, HOP_CUTS)),
        ],
        compiler_params=pltpu.CompilerParams(
            collective_id=0, has_side_effects=True, vmem_limit_bytes=50 * 1024 * 1024
        ),
    )(
        block_order, prompt_lengths, sink_logits[0],
        tokens, norm_gain, cosine, sine, w_key_value[0], w_query[0], w_out[0].T,
    )
    return hidden[None], cache[None]


def solution(mesh):
    in_specs = (
        P("groups", "seq", None),
        P("groups"),
        P("groups"),
        P("section", None),
        P("section", None, "seq"),
        P("section", None, None),
        P("section", "seq", None),
        P("section", None),
    )
    out_specs = (P("section", "groups", "seq", None), P("section", "groups", "seq", None))
    shape = tuple(mesh.shape[name] for name in ("groups", "section", "seq"))
    return jax.shard_map(
        functools.partial(per_device, shape),
        mesh=mesh, in_specs=in_specs, out_specs=out_specs, check_vma=False,
    )
```

profile of v0, /device:TPU:27, one launch (start us, length us, event | category | flops | bytes accessed | tf_op | source)
XLA Modules:
  0.0 105.5 jit_solution(5847665565379801713)
XLA Ops:
  0.7 0.2 fusion
  0.9 0.1 pad_maximum_fusion
  1.0 0.1 tile.9.cos_ref
  1.1 0.1 tile.21.sin_ref
  1.2 0.0 copy-start
  1.2 1.4 %copy-done = bf16[1,1440,512]{2,1,0:T(8,128)(2,1)S(1)} copy-done((bf16[1,1440,512]{2,1,0:T(8,128)(2,1)S(1)}, bf16[1,1440,512]{2,1,0:T(8,128)(2,1)}, u32[]{:S(2)}) %copy-start) | copy-done | bytes 1474584
  2.6 0.0 copy-start.1
  2.6 1.1 %copy-done.1 = bf16[4,64,1440]{2,1,0:T(8,128)(2,1)S(1)} copy-done((bf16[4,64,1440]{2,1,0:T(8,128)(2,1)S(1)}, bf16[4,64,1440]{2,1,0:T(8,128)(2,1)}, u32[]{:S(2)}) %copy-start.1) | copy-done | bytes 737304
  3.7 0.0 copy-start.2
  3.7 0.7 copy-done.2
  4.4 0.0 copy-start.3
  4.4 0.7 copy-done.3
  5.1 0.0 copy-start.4
  5.1 0.7 copy-done.4
  5.7 0.0 copy-start.5
  5.7 0.7 copy-done.5
  6.4 97.5 %shard_map.95 = (bf16[4,64,1440]{2,1,0:T(8,128)(2,1)S(1)}, bf16[4,64,512]{2,1,0:T(8,128)(2,1)S(1)}) custom-call(s32[4]{0:T(128)S(1)} %copy-done.3, s32[4]{0:T(128)S(1)} %copy-done.4, f32[32]{0:T(128)S(1)} %bitcast.11, bf16[4,64,1440]{2,1,0:T(8,128)(2,1)S(1)} %copy-done.1, f32[1,1440]{1,0:T(1,128)S(1)} %copy-done.2, f32[64,128]{1,0:T(8,128)S(1)} %tile.9.cos_ref, ...), custom_call_target="tpu_custom_call" | custom-call | tf_op jit(solution)/shard_map/pallas_call | solution.py:391
  103.9 0.9 copy.12
  104.8 0.7 copy.13
  (4 shorter events, 0.1 us)
Async XLA Ops:
  1.2 1.4 %copy-start = (bf16[1,1440,512]{2,1,0:T(8,128)(2,1)S(1)}, bf16[1,1440,512]{2,1,0:T(8,128)(2,1)}, u32[]{:S(2)}) copy-start(bf16[1,1440,512]{2,1,0:T(8,128)(2,1)} %param.13) | copy-start | bytes 4423684
  2.6 1.1 %copy-start.1 = (bf16[4,64,1440]{2,1,0:T(8,128)(2,1)S(1)}, bf16[4,64,1440]{2,1,0:T(8,128)(2,1)}, u32[]{:S(2)}) copy-start(bf16[4,64,1440]{2,1,0:T(8,128)(2,1)} %tokens_ref.1) | copy-start | bytes 2211844
  3.7 0.7 copy-start.2
  4.4 0.7 copy-start.3
  5.1 0.7 copy-start.4
  5.7 0.7 copy-start.5
where the time goes:
time: 106 us
  Pallas kernels  97.5 us (92%)
  local copies, waits for them, and re-layouts  7 us (7%)
    pallas_call x1, Pallas kernels, per_device(): pl.pallas_call(functools.partial(kernel, shape), out_shape=(jax.ShapeDtyp...  97.5 us
    unnamed x14, local copies, waits for them, and re-layouts  6.75 us

commit v1 on v0

v1 whole, which is shorter than its diff:
```python
import functools
import math

import jax
import jax.numpy as jnp
from jax import lax
from jax.experimental import pallas as pl
from jax.experimental.pallas import tpu as pltpu
from jax.sharding import PartitionSpec as P

HEAD_DIM = 64
WIN = 128
LANES = 128
THETA = 150000.0
EPSILON = 1e-05
MESH = pl.DeviceIdType.MESH
F32 = jnp.float32
BF16 = jnp.bfloat16
QUERY_CUTS = 5
OUT_STEP = 256
HOP_CUTS = 3


def kernel(
    shape,
    order_ref, length_ref, sink_ref,
    tokens_hbm, gain_hbm, pair_hbm, query_hbm, out_hbm,
    hidden_ref, cache_ref,
    tokens_ref, gain_ref, pair_ref, out_t, cos_tab, sin_tab,
    query_w, out_w, arrive, window, hbuf, normed_ref, qbuf, cbuf, sink_rows,
    gathered, tq, kd_buf, vd_buf, ctx, outgoing, incoming, final, acc,
    local_sem, x_send, x_recv, y_send, y_recv, d_send, d_recv, own_send, own_recv,
    w_send, w_recv, z_send, z_recv,
    ax_send, ax_recv, ad_send, ad_recv, rd_send, rd_recv, rx_send, rx_recv,
):
    groups, sections, seq = shape
    chips = seq // 2
    g = lax.axis_index("groups")
    sec = lax.axis_index("section")
    q = lax.axis_index("seq")
    chip, core = q // 2, q % 2
    partner = chip * 2 + (1 - core)
    micro, rows, width = hidden_ref.shape
    shard = query_w.shape[2]
    heads_width = seq * shard
    kv_width = pair_ref.shape[1] // 2
    kv_heads = kv_width // HEAD_DIM
    group = heads_width // kv_width
    keep = min(WIN, rows)
    depth = WIN // keep
    span = WIN + rows
    total = seq * rows
    half = HEAD_DIM // 2
    own_heads = shard // HEAD_DIM

    query_size = width // groups // QUERY_CUTS
    out_rows = shard // groups
    out_edges = [(c, min(OUT_STEP, width - c)) for c in range(0, width, OUT_STEP)]
    cuts = (QUERY_CUTS, len(out_edges))

    def query_load(j, k):
        first = pl.multiple_of((((g + j) % groups) * QUERY_CUTS + k) * query_size, 16)
        return pltpu.make_async_copy(
            query_hbm.at[pl.ds(first, query_size)], query_w.at[q, pl.ds(first, query_size)],
            local_sem.at[j * QUERY_CUTS + k],
        )

    base = groups * QUERY_CUTS
    out_load = pltpu.make_async_copy(out_hbm, out_t, local_sem.at[base])
    pair_load = pltpu.make_async_copy(pair_hbm, pair_ref, local_sem.at[base + 1])
    gain_load = pltpu.make_async_copy(gain_hbm, gain_ref, local_sem.at[base + 2])
    tokens_load = pltpu.make_async_copy(tokens_hbm, tokens_ref, local_sem.at[base + 3])

    @pl.when(sec == 0)
    def _():
        gain_load.start()
        tokens_load.start()

    for j in range(groups):
        for k in range(QUERY_CUTS):
            query_load(j, k).start()
    out_load.start()
    pair_load.start()

    @pl.when(sec > 0)
    def _():
        gain_load.start()

    barrier = pltpu.get_barrier_semaphore()
    greeted = 0
    for d in range(1, seq):
        pl.semaphore_signal(barrier, 1, device_id={"seq": (q + d) % seq}, device_id_type=MESH)
        greeted += 1
    for e in range(1, groups):
        pl.semaphore_signal(barrier, 1, device_id={"groups": (g + e) % groups}, device_id_type=MESH)
        greeted += 1
    for s in sorted({1 % sections, (sections - 1) % sections} - {0}):
        pl.semaphore_signal(barrier, 1, device_id={"section": (sec + s) % sections}, device_id_type=MESH)
        greeted += 1
    pl.semaphore_wait(barrier, greeted)

    def remote(src, dst, send, recv, target):
        return pltpu.make_async_remote_copy(
            src_ref=src, dst_ref=dst, send_sem=send, recv_sem=recv,
            device_id=target, device_id_type=MESH,
        )

    def source(d, which):
        return ((chip - d + chips) % chips) * 2 + which

    def ahead(d, which):
        return ((chip + d) % chips) * 2 + which

    def own_rows(owner):
        return pl.ds(pl.multiple_of(owner * shard, shard), shard)

    def piece(kind, owner, part, k):
        if kind == 0:
            first = (part * QUERY_CUTS + k) * query_size
            return query_w.at[owner, pl.ds(pl.multiple_of(first, 16), query_size)]
        first = pl.multiple_of(owner * shard + part * out_rows, out_rows)
        return out_w.at[pl.ds(first, out_rows), pl.ds(*out_edges[k])]

    def whole(kind, owner):
        if kind == 0:
            return query_w.at[owner]
        return out_w.at[own_rows(owner)]

    def x_copy(kind, d, k, owner):
        ref = piece(kind, owner, g, k)
        return remote(ref, ref, x_send.at[kind, d, k], x_recv.at[kind, d, k], {"seq": ahead(d, core)})

    def y_copy(kind, d, k, e, owner, part):
        ref = piece(kind, owner, part, k)
        return remote(
            ref, ref, y_send.at[kind, d, k, e], y_recv.at[kind, d, k, e], {"groups": (g + e) % groups}
        )

    def d_copy(kind, d, k, e, owner):
        ref = piece(kind, owner, (g - e + groups) % groups, k)
        return remote(ref, ref, d_send.at[kind, d, k, e], d_recv.at[kind, d, k, e], {"seq": partner})

    def own_copy(kind, owner):
        ref = whole(kind, owner)
        return remote(ref, ref, own_send.at[kind], own_recv.at[kind], {"seq": partner})

    step = -(-width // (HOP_CUTS * LANES)) * LANES
    edges = [(c * step, min(step, width - c * step)) for c in range(HOP_CUTS)]

    def z_copy(t, c):
        columns = pl.ds(*edges[c])
        return remote(
            hidden_ref.at[t, :, columns], arrive.at[t, :, columns],
            z_send.at[t, c], z_recv.at[t, c], {"section": (sec + 1) % sections},
        )

    def w_copy(t, off, side):
        columns = pl.ds(side * kv_width, kv_width)
        return remote(
            cache_ref.at[t, pl.ds(rows - keep, keep), columns], window.at[t, off - 1, :, columns],
            w_send.at[t, off - 1, side], w_recv.at[t, off - 1, side], {"seq": (q + off) % seq},
        )

    def ax_copy(t, d, owner):
        ref = gathered.at[t, owner]
        return remote(ref, ref, ax_send.at[t, d], ax_recv.at[t, d], {"seq": ahead(d, core)})

    def ad_copy(t, d, owner):
        ref = gathered.at[t, owner]
        return remote(ref, ref, ad_send.at[t, d], ad_recv.at[t, d], {"seq": partner})

    def rd_copy(t, d):
        return remote(
            outgoing.at[t, d], incoming.at[t, d], rd_send.at[t, d], rd_recv.at[t, d], {"seq": partner}
        )

    def rx_copy(t, d, c):
        columns = pl.ds(*edges[c])
        return remote(
            incoming.at[t, d, :, columns], final.at[t, d, :, columns],
            rx_send.at[t, d, c], rx_recv.at[t, d, c], {"seq": ahead(d, core)},
        )

    def tables(r):
        lane = lax.broadcasted_iota(jnp.int32, (rows, LANES), 1)
        place = lax.broadcasted_iota(jnp.int32, (rows, LANES), 0) + r * rows
        freq = jnp.exp((lane % half).astype(F32) * (-2.0 * math.log(THETA) / HEAD_DIM))
        angles = place.astype(F32) * freq
        at = pl.ds(pl.multiple_of(r * rows, rows), rows)
        cos_tab[at] = jnp.cos(angles)
        sine = jnp.sin(angles)
        sin_tab[at] = jnp.where((lane % HEAD_DIM) < half, -sine, sine)

    def rotate(tile, cosine, sine):
        lane = lax.broadcasted_iota(jnp.int32, tile.shape, 1)
        first_half = (lane % HEAD_DIM) < half
        swapped = jnp.where(
            first_half, pltpu.roll(tile, LANES - half, 1), pltpu.roll(tile, half, 1)
        )
        return tile * cosine + swapped * sine

    def norm(h):
        widened = h.astype(F32)
        scale = lax.rsqrt(jnp.mean(widened * widened, -1, keepdims=True) + EPSILON)
        return (widened * scale * gain_ref[...]).astype(BF16)

    def transpose_out():
        out_load.wait()
        for first in range(0, width, LANES):
            size = min(LANES, width - first)
            out_w[own_rows(q), first:first + size] = out_t[first:first + size, :].T

    def bias_of(r, length, lanes):
        key = lax.broadcasted_iota(jnp.int32, (span, lanes), 0) - WIN
        row = lax.broadcasted_iota(jnp.int32, (span, lanes), 1) % rows
        column = key + r * rows
        allowed = (key <= row) & (row - key < WIN) & (column >= 0)
        allowed = allowed & ((column < length) | (key == row))
        return jnp.where(allowed, F32(0.0), F32(-1e30))

    def sink_row(first, tiles):
        return jnp.concatenate(
            [jnp.full((1, rows), sink_ref[first + 2 * p], F32) for p in range(tiles)], 1
        )

    low = lax.broadcasted_iota(jnp.int32, (span, LANES), 1) < HEAD_DIM
    ones = jnp.ones((16, span), BF16)

    def attention(pairs, twice, values_t, bias, sinks):
        zero = jnp.zeros_like(twice)
        sides = jnp.concatenate([jnp.where(low, twice, zero), jnp.where(low, zero, twice)], 0)
        scores = lax.dot_general(
            sides, jnp.concatenate(pairs, 0), (((1,), (1,)), ((), ())), preferred_element_type=F32
        )
        extended = jnp.concatenate([values_t, ones], 0)
        parts = []
        for b in range(2):
            masked = scores[b * span:(b + 1) * span] + bias
            top = jnp.maximum(jnp.max(masked, 0, keepdims=True), sinks[b])
            expo = jnp.exp(masked - top).astype(BF16)
            summed = jnp.dot(extended, expo, preferred_element_type=F32)
            whole_sum = summed[HEAD_DIM:HEAD_DIM + 1] + jnp.exp(sinks[b] - top)
            parts.append(summed[:HEAD_DIM] * (1.0 / whole_sum))
        return jnp.concatenate(parts, 0).T.astype(BF16)

    def cache_of(t, normed, cosine, sine, send):
        keys = jnp.dot(normed, pair_ref[:, :kv_width], preferred_element_type=F32)
        for p in range(kv_width // LANES):
            tile = slice(p * LANES, (p + 1) * LANES)
            cache_ref[t, :, tile] = rotate(keys[:, tile], cosine, sine).astype(BF16)
        if send:
            for off in range(1, depth + 1):

                @pl.when(q + off < seq)
                def _():
                    w_copy(t, off, 0).start()

        values = jnp.dot(normed, pair_ref[:, kv_width:], preferred_element_type=F32)
        cache_ref[t, :, kv_width:] = values.astype(BF16)
        if send:
            for off in range(1, depth + 1):

                @pl.when(q + off < seq)
                def _():
                    w_copy(t, off, 1).start()

    mine = pl.ds(pl.multiple_of(q * rows, rows), rows)

    def first_section():
        tiles = shard // LANES
        gain_load.wait()
        tokens_load.wait()
        for t in range(micro):
            hbuf[t] = tokens_ref[order_ref[t]]
            gathered[t, q] = norm(hbuf[t])
            if t < micro - 1 or micro < 3:
                for d in range(1, chips):
                    ax_copy(t, d, q).start()
            ad_copy(t, 0, q).start()
        for r in range(seq):
            tables(r)
        kd_buf[:WIN] = jnp.zeros((WIN, LANES), BF16)
        vd_buf[:WIN] = jnp.zeros((WIN, LANES), BF16)
        transpose_out()
        pair_load.wait()
        for j in range(groups):
            for k in range(QUERY_CUTS):
                query_load(j, k).wait()
        for t in range(micro):
            cache_of(t, gathered[t, q], cos_tab[mine], sin_tab[mine], False)

        kv_head = (q * own_heads) // group
        pair_at = pl.ds(pl.multiple_of((kv_head // 2) * LANES, LANES), LANES)
        value_at = pl.ds(pl.multiple_of(kv_width + (kv_head // 2) * LANES, LANES), LANES)
        sinks = [sink_row(q * own_heads + b, tiles) for b in range(2)]

        def double(tile):
            lane = lax.broadcasted_iota(jnp.int32, tile.shape, 1)
            kept = jnp.where(lane // HEAD_DIM == kv_head % 2, tile, 0.0)
            return (kept + pltpu.roll(kept, HEAD_DIM, 1)).astype(BF16)

        def compute(t):
            for d in range(1, chips):
                ax_copy(t, d, source(d, core)).wait_recv()
                ad_copy(t, d, source(d, core)).start()
            for d in range(chips):
                ad_copy(t, d, source(d, 1 - core)).wait_recv()
            length = length_ref[order_ref[t]]
            normed = gathered[t].reshape(total, width)
            cosine, sine = cos_tab[...], sin_tab[...]
            keys = jnp.dot(normed, pair_ref[:, pair_at], preferred_element_type=F32)
            kd_buf[WIN:] = double(rotate(keys, cosine, sine))
            vd_buf[WIN:] = double(jnp.dot(normed, pair_ref[:, value_at], preferred_element_type=F32))
            queries = jnp.dot(normed, query_w[q], preferred_element_type=F32)
            for p in range(tiles):
                tile = slice(p * LANES, (p + 1) * LANES)
                tq[:, tile] = (rotate(queries[:, tile], cosine, sine) * 0.125).astype(BF16)
            for r in range(seq):
                at = slice(r * rows, r * rows + span)
                some = attention(
                    [tq[r * rows:(r + 1) * rows, p * LANES:(p + 1) * LANES] for p in range(tiles)],
                    kd_buf[at], vd_buf[at].T[:HEAD_DIM], bias_of(r, length, tiles * rows), sinks,
                )
                for p in range(tiles):
                    ctx[r, :, p * LANES:(p + 1) * LANES] = some[p * rows:(p + 1) * rows]
            weights = out_w[own_rows(q), :]
            there = jnp.dot(
                jnp.concatenate([ctx[ahead(d, 1 - core)] for d in range(chips)], 0), weights,
                preferred_element_type=F32,
            )
            for d in list(range(1, chips)) + [0]:
                outgoing[t, d] = there[d * rows:(d + 1) * rows].astype(BF16)
                rd_copy(t, d).start()
            here = jnp.dot(
                jnp.concatenate([ctx[ahead(d, core)] for d in range(chips)], 0), weights,
                preferred_element_type=F32,
            )
            acc[t] = hbuf[t].astype(F32) + here[:rows]
            for d in range(1, chips):
                rd_copy(t, d).wait_recv()
                joined = here[d * rows:(d + 1) * rows] + incoming[t, d].astype(F32)
                incoming[t, d] = joined.astype(BF16)
                for c in range(HOP_CUTS):
                    rx_copy(t, d, c).start()

        def finish(t):
            rd_copy(t, 0).wait_recv()
            for c, (first, size) in enumerate(edges):
                columns = slice(first, first + size)
                joined = acc[t, :, columns] + incoming[t, 0, :, columns].astype(F32)
                for d in range(1, chips):
                    rx_copy(t, d, c).wait_recv()
                    joined = joined + final[t, d, :, columns].astype(F32)
                hidden_ref[t, :, columns] = joined.astype(BF16)
                if sections > 1:
                    z_copy(t, c).start()

        @pl.loop(0, micro)
        def _(t):
            if micro >= 3:

                @pl.when(t == micro - 1)
                def _():
                    finish(0)

            compute(t)
            if micro >= 3:

                @pl.when(t == 0)
                def _():
                    for d in range(1, chips):
                        ax_copy(micro - 1, d, q).start()

        @pl.loop(1 if micro >= 3 else 0, micro)
        def _(t):
            finish(t)

        for t in range(micro):
            for d in range(1, chips):
                ax_copy(t, d, q).wait_send()
                for c in range(HOP_CUTS):
                    rx_copy(t, d, c).wait_send()
            for d in range(chips):
                ad_copy(t, d, source(d, core)).wait_send()
                rd_copy(t, d).wait_send()

    def later_section():
        tiles = group // 2
        plan = [(kind, k, d) for kind in range(2) for k in range(cuts[kind]) for d in range(1, chips)]
        for k in range(QUERY_CUTS):
            query_load(0, k).wait()
            for d in range(1, chips):
                x_copy(0, d, k, q).start()
        transpose_out()
        for k in range(cuts[1]):
            for d in range(1, chips):
                x_copy(1, d, k, q).start()
        for j in range(1, groups):
            for k in range(QUERY_CUTS):
                query_load(j, k).wait()
        for kind in range(2):
            own_copy(kind, q).start()
        tables(q)
        for off in range(1, depth + 1):

            @pl.when(q < off)
            def _():
                window[:, off - 1] = jnp.zeros((micro, keep, 2 * kv_width), BF16)

        for h in range(kv_heads):
            for b in range(2):
                sink_rows[2 * h + b:2 * h + b + 1, :] = sink_row(h * group + b, tiles)
        gain_load.wait()
        pair_load.wait()

        def relay_y(kind, k, d):
            for e in range(1, groups):
                y_copy(kind, d, k, e, source(d, core), (g - e + groups) % groups).wait_recv()
                d_copy(kind, d, k, e, source(d, core)).start()

        previous = None
        for kind, k, d in plan:
            x_copy(kind, d, k, source(d, core)).wait_recv()
            for e in range(1, groups):
                y_copy(kind, d, k, e, source(d, core), g).start()
            d_copy(kind, d, k, 0, source(d, core)).start()
            if previous is not None:
                relay_y(*previous)
            previous = (kind, k, d)
        if previous is not None:
            relay_y(*previous)
        for kind in range(2):
            own_copy(kind, partner).wait_recv()
        for kind, k, d in plan:
            for e in range(groups):
                d_copy(kind, d, k, e, source(d, 1 - core)).wait_recv()

        def enter(t):
            for c in range(HOP_CUTS):
                z_copy(t, c).wait_recv()
            normed_ref[t] = norm(arrive[t])
            cache_of(t, normed_ref[t], cos_tab[mine], sin_tab[mine], True)

        def attend(t):
            length = length_ref[order_ref[t]]
            normed = normed_ref[t]
            cosine, sine = cos_tab[mine], sin_tab[mine]
            for s in range(seq):
                queries = jnp.dot(normed, query_w[s], preferred_element_type=F32)
                for p in range(shard // LANES):
                    rotated = rotate(queries[:, p * LANES:(p + 1) * LANES], cosine, sine) * 0.125
                    qbuf[:, s * shard + p * LANES:s * shard + (p + 1) * LANES] = rotated.astype(BF16)
            for off in range(1, depth + 1):

                @pl.when(q >= off)
                def _():
                    w_copy(t, off, 0).wait_recv()
                    w_copy(t, off, 1).wait_recv()

            bias = bias_of(q, length, tiles * rows)

            def span_of(first, size):
                at = slice(first, first + size)
                parts = [window[t, off - 1, :, at] for off in range(depth, 0, -1)]
                return jnp.concatenate(parts + [cache_ref[t, :, at]], 0)

            for pair in range(kv_heads // 2):
                values_t = span_of(kv_width + pair * LANES, LANES).T
                for e in range(2):
                    h = pair * 2 + e
                    head = span_of(h * HEAD_DIM, HEAD_DIM)
                    at = [(h * tiles + p) * LANES for p in range(tiles)]
                    some = attention(
                        [qbuf[:, a:a + LANES] for a in at], jnp.concatenate([head, head], 1),
                        values_t[e * HEAD_DIM:(e + 1) * HEAD_DIM], bias,
                        [sink_rows[2 * h + b:2 * h + b + 1, :] for b in range(2)],
                    )
                    for p in range(tiles):
                        cbuf[:, at[p]:at[p] + LANES] = some[p * rows:(p + 1) * rows]

        def slot(t, carry):
            enter(t)
            attend(t)
            for c, (first, size) in enumerate(edges):
                columns = slice(first, first + size)
                output = jnp.dot(cbuf[...], out_w[:, columns], preferred_element_type=F32)
                hidden_ref[t, :, columns] = (arrive[t, :, columns].astype(F32) + output).astype(BF16)

                @pl.when(sec + 1 < sections)
                def _():
                    z_copy(t, c).start()

            return carry

        lax.fori_loop(0, micro, slot, 0)

        for kind, k, d in plan:
            x_copy(kind, d, k, q).wait_send()
            for e in range(1, groups):
                y_copy(kind, d, k, e, source(d, core), g).wait_send()
            for e in range(groups):
                d_copy(kind, d, k, e, source(d, core)).wait_send()
        for kind in range(2):
            own_copy(kind, q).wait_send()
        for t in range(micro):
            for off in range(1, depth + 1):

                @pl.when(q + off < seq)
                def _():
                    w_copy(t, off, 0).wait_send()
                    w_copy(t, off, 1).wait_send()


    @pl.when(sec == 0)
    def _():
        first_section()

    @pl.when(sec > 0)
    def _():
        later_section()

    @pl.when(sec + 1 < sections)
    def _():
        for t in range(micro):
            for c in range(HOP_CUTS):
                z_copy(t, c).wait_send()


def per_device(
    shape,
    tokens, block_order, prompt_lengths, norm_gain, w_query, w_key_value, w_out, sink_logits
):
    groups, sections, seq = shape
    micro, rows, width = tokens.shape
    shard = w_query.shape[2]
    pair_width = w_key_value.shape[2]
    kv_heads = pair_width // 2 // HEAD_DIM
    lanes = seq * shard // (pair_width // 2) // 2 * rows
    chips = seq // 2
    keep = min(WIN, rows)
    depth = WIN // keep
    most = max(QUERY_CUTS, -(-width // OUT_STEP))
    limit = (52 if seq * rows <= 512 else 57) * 1024 * 1024
    dma = pltpu.SemaphoreType.DMA
    vmem = pl.BlockSpec(memory_space=pltpu.VMEM)
    smem = pl.BlockSpec(memory_space=pltpu.SMEM)
    hbm = pl.BlockSpec(memory_space=pltpu.HBM)
    hidden, cache = pl.pallas_call(
        functools.partial(kernel, shape),
        out_shape=(
            jax.ShapeDtypeStruct((micro, rows, width), BF16),
            jax.ShapeDtypeStruct((micro, rows, pair_width), BF16),
        ),
        in_specs=[smem] * 3 + [hbm] * 5,
        out_specs=(vmem, vmem),
        scratch_shapes=[
            pltpu.VMEM((micro, rows, width), BF16),
            pltpu.VMEM((1, width), F32),
            pltpu.VMEM((width, pair_width), BF16),
            pltpu.VMEM((width, shard), BF16),
            pltpu.VMEM((seq * rows, LANES), F32),
            pltpu.VMEM((seq * rows, LANES), F32),
            pltpu.VMEM((seq, width, shard), BF16),
            pltpu.VMEM((seq * shard, width), BF16),
            pltpu.VMEM((micro, rows, width), BF16),
            pltpu.VMEM((micro, depth, keep, pair_width), BF16),
            pltpu.VMEM((micro, rows, width), BF16),
            pltpu.VMEM((micro, rows, width), BF16),
            pltpu.VMEM((rows, seq * shard), BF16),
            pltpu.VMEM((rows, seq * shard), BF16),
            pltpu.VMEM((2 * kv_heads, lanes), F32),
            pltpu.VMEM((micro, seq, rows, width), BF16),
            pltpu.VMEM((seq * rows, shard), BF16),
            pltpu.VMEM((WIN + seq * rows, LANES), BF16),
            pltpu.VMEM((WIN + seq * rows, LANES), BF16),
            pltpu.VMEM((seq, rows, shard), BF16),
            pltpu.VMEM((micro, chips, rows, width), BF16),
            pltpu.VMEM((micro, chips, rows, width), BF16),
            pltpu.VMEM((micro, chips, rows, width), BF16),
            pltpu.VMEM((micro, rows, width), F32),
            dma((groups * QUERY_CUTS + 4,)),
            dma((2, chips, most)),
            dma((2, chips, most)),
            dma((2, chips, most, groups)),
            dma((2, chips, most, groups)),
            dma((2, chips, most, groups)),
            dma((2, chips, most, groups)),
            dma((2,)),
            dma((2,)),
            dma((micro, depth, 2)),
            dma((micro, depth, 2)),
            dma((micro, HOP_CUTS)),
            dma((micro, HOP_CUTS)),
            dma((micro, chips)),
            dma((micro, chips)),
            dma((micro, chips)),
            dma((micro, chips)),
            dma((micro, chips)),
            dma((micro, chips)),
            dma((micro, chips, HOP_CUTS)),
            dma((micro, chips, HOP_CUTS)),
        ],
        compiler_params=pltpu.CompilerParams(
            collective_id=0, has_side_effects=True, vmem_limit_bytes=limit
        ),
    )(
        block_order, prompt_lengths, sink_logits[0],
        tokens, norm_gain, w_key_value[0], w_query[0], w_out[0].T,
    )
    return hidden[None], cache[None]


def solution(mesh):
    in_specs = (
        P("groups", "seq", None),
        P("groups"),
        P("groups"),
        P("section", None),
        P("section", None, "seq"),
        P("section", None, None),
        P("section", "seq", None),
        P("section", None),
    )
    out_specs = (P("section", "groups", "seq", None), P("section", "groups", "seq", None))
    shape = tuple(mesh.shape[name] for name in ("groups", "section", "seq"))
    return jax.shard_map(
        functools.partial(per_device, shape),
        mesh=mesh, in_specs=in_specs, out_specs=out_specs, check_vma=False,
    )
```

time: 106 us -> 92.2 us (0.87)
  Pallas kernels: 97.5 us -> 86 us
  local copies, waits for them, and re-layouts: 7 us -> 5.37 us
    pallas_call x1, Pallas kernels: 97.5 us -> 86 us  [per_device(): pl.pallas_call(functools.partial(kernel, shape), out_shape=(jax.ShapeDtyp...]
    unnamed x14 -> x12, local copies, waits for them, and re-layouts: 6.75 us -> 5.37 us
where the time goes in v1:
time: 92.2 us; the launch traced here: 92 us
  Pallas kernels  86 us (93%)
  local copies, waits for them, and re-layouts  5.37 us (6%)
    pallas_call x1, Pallas kernels, per_device(): pl.pallas_call(functools.partial(kernel, shape), out_shape=(jax.ShapeDtyp...  86 us
    unnamed x12, local copies, waits for them, and re-layouts  5.37 us

profile of v1, /device:TPU:27, one launch (start us, length us, event | category | flops | bytes accessed | tf_op | source)
XLA Modules:
  0.0 92.0 jit_solution(2032064347874971725)
XLA Ops:
  0.6 0.0 copy-start
  0.6 1.1 %copy-done = bf16[4,64,1440]{2,1,0:T(8,128)(2,1)S(1)} copy-done((bf16[4,64,1440]{2,1,0:T(8,128)(2,1)S(1)}, bf16[4,64,1440]{2,1,0:T(8,128)(2,1)}, u32[]{:S(2)}) %copy-start) | copy-done | bytes 737304
  1.8 0.0 copy-start.1
  1.8 0.7 copy-done.1
  2.5 0.0 copy-start.2
  2.5 0.7 copy-done.2
  3.1 0.0 copy-start.3
  3.1 0.7 copy-done.3
  3.8 0.0 copy-start.4
  3.8 0.7 copy-done.4
  4.4 86.0 %shard_map.95 = (bf16[4,64,1440]{2,1,0:T(8,128)(2,1)S(1)}, bf16[4,64,512]{2,1,0:T(8,128)(2,1)S(1)}) custom-call(s32[4]{0:T(128)S(1)} %copy-done.2, s32[4]{0:T(128)S(1)} %copy-done.3, f32[32]{0:T(128)S(1)} %bitcast.10, bf16[4,64,1440]{2,1,0:T(8,128)(2,1)S(1)} %copy-done, f32[1,1440]{1,0:T(1,128)S(1)} %copy-done.1, bf16[1440,512]{1,0:T(8,128)(2,1)} %bitcast.11, ...), custom_call_target="tpu_custom_call" | custom-call | tf_op jit(solution)/shard_map/pallas_call | solution.py:548
  90.4 0.9 copy.12
  91.3 0.7 copy.13
Async XLA Ops:
  0.6 1.1 %copy-start = (bf16[4,64,1440]{2,1,0:T(8,128)(2,1)S(1)}, bf16[4,64,1440]{2,1,0:T(8,128)(2,1)}, u32[]{:S(2)}) copy-start(bf16[4,64,1440]{2,1,0:T(8,128)(2,1)} %tokens_hbm.1) | copy-start | bytes 2211844
  1.8 0.7 copy-start.1
  2.5 0.7 copy-start.2
  3.1 0.7 copy-start.3
  3.8 0.7 copy-start.4

commit v2 on v1

--- a/solution.py
+++ b/solution.py
@@ -19,14 +19,24 @@
 QUERY_CUTS = 5
 OUT_STEP = 256
 HOP_CUTS = 3
+SECOND_ORDER = "e0 f q0 r f r f f a0 w0 o00 r e1 r q1 w1 o01 r f w2 o02 a1 o10 o11 o12"
+AHEAD = 2
+
+
+def out_pieces(width):
+    direct = width % LANES + LANES
+    coarse = (width - direct) // OUT_STEP * OUT_STEP
+    edges = [(c, OUT_STEP) for c in range(0, coarse - OUT_STEP, OUT_STEP)]
+    edges += [(c, LANES) for c in range(coarse - OUT_STEP, width - direct, LANES)]
+    return edges + [(width - direct, direct)]
 
 
 def kernel(
     shape,
-    order_ref, length_ref, sink_ref,
-    tokens_hbm, gain_hbm, pair_hbm, query_hbm, out_hbm,
+    whole_ref, real_ref, real_row,
+    tokens_hbm, pair_hbm, query_hbm, out_hbm,
     hidden_ref, cache_ref,
-    tokens_ref, gain_ref, pair_ref, out_t, cos_tab, sin_tab,
+    tokens_ref, pair_ref, out_t, cos_tab, sin_tab,
     query_w, out_w, arrive, window, hbuf, normed_ref, qbuf, cbuf, sink_rows,
     gathered, tq, kd_buf, vd_buf, ctx, outgoing, incoming, final, acc,
     local_sem, x_send, x_recv, y_send, y_recv, d_send, d_recv, own_send, own_recv,
@@ -55,8 +65,9 @@
 
     query_size = width // groups // QUERY_CUTS
     out_rows = shard // groups
-    out_edges = [(c, min(OUT_STEP, width - c)) for c in range(0, width, OUT_STEP)]
-    cuts = (QUERY_CUTS, len(out_edges))
+    out_edges = out_pieces(width)
+    last_edge = out_edges[-1]
+    cuts = (QUERY_CUTS, len(out_edges) - 1, 1)
 
     def query_load(j, k):
         first = pl.multiple_of((((g + j) % groups) * QUERY_CUTS + k) * query_size, 16)
@@ -68,12 +79,10 @@
     base = groups * QUERY_CUTS
     out_load = pltpu.make_async_copy(out_hbm, out_t, local_sem.at[base])
     pair_load = pltpu.make_async_copy(pair_hbm, pair_ref, local_sem.at[base + 1])
-    gain_load = pltpu.make_async_copy(gain_hbm, gain_ref, local_sem.at[base + 2])
-    tokens_load = pltpu.make_async_copy(tokens_hbm, tokens_ref, local_sem.at[base + 3])
+    tokens_load = pltpu.make_async_copy(tokens_hbm, tokens_ref, local_sem.at[base + 2])
 
     @pl.when(sec == 0)
     def _():
-        gain_load.start()
         tokens_load.start()
 
     for j in range(groups):
@@ -81,10 +90,6 @@
             query_load(j, k).start()
     out_load.start()
     pair_load.start()
-
-    @pl.when(sec > 0)
-    def _():
-        gain_load.start()
 
     barrier = pltpu.get_barrier_semaphore()
     greeted = 0
@@ -118,6 +123,8 @@
         if kind == 0:
             first = (part * QUERY_CUTS + k) * query_size
             return query_w.at[owner, pl.ds(pl.multiple_of(first, 16), query_size)]
+        if kind == 2:
+            return out_w.at[own_rows(owner), pl.ds(*last_edge)]
         first = pl.multiple_of(owner * shard + part * out_rows, out_rows)
         return out_w.at[pl.ds(first, out_rows), pl.ds(*out_edges[k])]
 
@@ -126,19 +133,36 @@
             return query_w.at[owner]
         return out_w.at[own_rows(owner)]
 
+    slots = (0, cuts[0], cuts[0] + cuts[1])
+
     def x_copy(kind, d, k, owner):
         ref = piece(kind, owner, g, k)
-        return remote(ref, ref, x_send.at[kind, d, k], x_recv.at[kind, d, k], {"seq": ahead(d, core)})
+        return remote(ref, ref, x_send.at[kind, d - 1], x_recv.at[d - 1, slots[kind] + k], {"seq": ahead(d, core)})
 
     def y_copy(kind, d, k, e, owner, part):
         ref = piece(kind, owner, part, k)
         return remote(
-            ref, ref, y_send.at[kind, d, k, e], y_recv.at[kind, d, k, e], {"groups": (g + e) % groups}
+            ref, ref, y_send.at[kind, d - 1, e - 1], y_recv.at[d - 1, slots[kind] + k, e - 1], {"groups": (g + e) % groups}
         )
 
     def d_copy(kind, d, k, e, owner):
         ref = piece(kind, owner, (g - e + groups) % groups, k)
-        return remote(ref, ref, d_send.at[kind, d, k, e], d_recv.at[kind, d, k, e], {"seq": partner})
+        return remote(ref, ref, d_send.at[kind], d_recv.at[0 if kind == 0 else slots[kind] - slots[1] + 1 + k], {"seq": partner})
+
+    def part_of(kind, owner, part):
+        if kind == 0:
+            size = QUERY_CUTS * query_size
+            return query_w.at[owner, pl.ds(pl.multiple_of(part * size, 16), size)]
+        if kind == 2:
+            return piece(2, owner, part, 0)
+        first = pl.multiple_of(owner * shard + part * out_rows, out_rows)
+        return out_w.at[pl.ds(first, out_rows), pl.ds(0, last_edge[0])]
+
+    def sent(ref, sem):
+        remote(ref, ref, sem, sem, {"seq": partner}).wait_send()
+
+    def landed(ref, sem):
+        remote(ref, ref, sem, sem, {"seq": partner}).wait_recv()
 
     def own_copy(kind, owner):
         ref = whole(kind, owner)
@@ -151,34 +175,33 @@
         columns = pl.ds(*edges[c])
         return remote(
             hidden_ref.at[t, :, columns], arrive.at[t, :, columns],
-            z_send.at[t, c], z_recv.at[t, c], {"section": (sec + 1) % sections},
-        )
-
-    def w_copy(t, off, side):
-        columns = pl.ds(side * kv_width, kv_width)
+            z_send.at[0], z_recv.at[t], {"section": (sec + 1) % sections},
+        )
+
+    def w_copy(t, off):
         return remote(
-            cache_ref.at[t, pl.ds(rows - keep, keep), columns], window.at[t, off - 1, :, columns],
-            w_send.at[t, off - 1, side], w_recv.at[t, off - 1, side], {"seq": (q + off) % seq},
+            cache_ref.at[t, pl.ds(rows - keep, keep)], window.at[t, off - 1],
+            w_send.at[off - 1], w_recv.at[t, off - 1], {"seq": (q + off) % seq},
         )
 
     def ax_copy(t, d, owner):
         ref = gathered.at[t, owner]
-        return remote(ref, ref, ax_send.at[t, d], ax_recv.at[t, d], {"seq": ahead(d, core)})
+        return remote(ref, ref, ax_send.at[d - 1], ax_recv.at[t, d - 1], {"seq": ahead(d, core)})
 
     def ad_copy(t, d, owner):
         ref = gathered.at[t, owner]
-        return remote(ref, ref, ad_send.at[t, d], ad_recv.at[t, d], {"seq": partner})
+        return remote(ref, ref, ad_send.at[0], ad_recv.at[t], {"seq": partner})
 
     def rd_copy(t, d):
         return remote(
-            outgoing.at[t, d], incoming.at[t, d], rd_send.at[t, d], rd_recv.at[t, d], {"seq": partner}
+            outgoing.at[t, d], incoming.at[t, d], rd_send.at[0], rd_recv.at[t, d], {"seq": partner}
         )
 
     def rx_copy(t, d, c):
         columns = pl.ds(*edges[c])
         return remote(
             incoming.at[t, d, :, columns], final.at[t, d, :, columns],
-            rx_send.at[t, d, c], rx_recv.at[t, d, c], {"seq": ahead(d, core)},
+            rx_send.at[d - 1], rx_recv.at[t, d - 1, c], {"seq": ahead(d, core)},
         )
 
     def tables(r):
@@ -202,7 +225,7 @@
     def norm(h):
         widened = h.astype(F32)
         scale = lax.rsqrt(jnp.mean(widened * widened, -1, keepdims=True) + EPSILON)
-        return (widened * scale * gain_ref[...]).astype(BF16)
+        return (widened * scale * real_row[:, :width]).astype(BF16)
 
     def transpose_out():
         out_load.wait()
@@ -220,7 +243,7 @@
 
     def sink_row(first, tiles):
         return jnp.concatenate(
-            [jnp.full((1, rows), sink_ref[first + 2 * p], F32) for p in range(tiles)], 1
+            [jnp.full((1, rows), real_ref[0, width + first + 2 * p], F32) for p in range(tiles)], 1
         )
 
     low = lax.broadcasted_iota(jnp.int32, (span, LANES), 1) < HEAD_DIM
@@ -248,13 +271,6 @@
         for p in range(kv_width // LANES):
             tile = slice(p * LANES, (p + 1) * LANES)
             cache_ref[t, :, tile] = rotate(keys[:, tile], cosine, sine).astype(BF16)
-        if send:
-            for off in range(1, depth + 1):
-
-                @pl.when(q + off < seq)
-                def _():
-                    w_copy(t, off, 0).start()
-
         values = jnp.dot(normed, pair_ref[:, kv_width:], preferred_element_type=F32)
         cache_ref[t, :, kv_width:] = values.astype(BF16)
         if send:
@@ -262,16 +278,15 @@
 
                 @pl.when(q + off < seq)
                 def _():
-                    w_copy(t, off, 1).start()
+                    w_copy(t, off).start()
 
     mine = pl.ds(pl.multiple_of(q * rows, rows), rows)
 
     def first_section():
         tiles = shard // LANES
-        gain_load.wait()
         tokens_load.wait()
         for t in range(micro):
-            hbuf[t] = tokens_ref[order_ref[t]]
+            hbuf[t] = tokens_ref[whole_ref[t]]
             gathered[t, q] = norm(hbuf[t])
             if t < micro - 1 or micro < 3:
                 for d in range(1, chips):
@@ -299,13 +314,24 @@
             kept = jnp.where(lane // HEAD_DIM == kv_head % 2, tile, 0.0)
             return (kept + pltpu.roll(kept, HEAD_DIM, 1)).astype(BF16)
 
+        def finish(t):
+            rd_copy(t, 0).wait_recv()
+            for c, (first, size) in enumerate(edges):
+                columns = slice(first, first + size)
+                joined = acc[t, :, columns] + incoming[t, 0, :, columns].astype(F32)
+                for d in range(1, chips):
+                    rx_copy(t, d, c).wait_recv()
+                    joined = joined + final[t, d, :, columns].astype(F32)
+                hidden_ref[t, :, columns] = joined.astype(BF16)
+                if sections > 1:
+                    z_copy(t, c).start()
+
         def compute(t):
             for d in range(1, chips):
                 ax_copy(t, d, source(d, core)).wait_recv()
                 ad_copy(t, d, source(d, core)).start()
-            for d in range(chips):
-                ad_copy(t, d, source(d, 1 - core)).wait_recv()
-            length = length_ref[order_ref[t]]
+            landed(outgoing.at[t], ad_recv.at[t])
+            length = whole_ref[micro + whole_ref[t]]
             normed = gathered[t].reshape(total, width)
             cosine, sine = cos_tab[...], sin_tab[...]
             keys = jnp.dot(normed, pair_ref[:, pair_at], preferred_element_type=F32)
@@ -323,6 +349,12 @@
                 )
                 for p in range(tiles):
                     ctx[r, :, p * LANES:(p + 1) * LANES] = some[p * rows:(p + 1) * rows]
+            if micro >= 3:
+
+                @pl.when(t == micro - 1)
+                def _():
+                    finish(1)
+
             weights = out_w[own_rows(q), :]
             there = jnp.dot(
                 jnp.concatenate([ctx[ahead(d, 1 - core)] for d in range(chips)], 0), weights,
@@ -343,23 +375,11 @@
                 for c in range(HOP_CUTS):
                     rx_copy(t, d, c).start()
 
-        def finish(t):
-            rd_copy(t, 0).wait_recv()
-            for c, (first, size) in enumerate(edges):
-                columns = slice(first, first + size)
-                joined = acc[t, :, columns] + incoming[t, 0, :, columns].astype(F32)
-                for d in range(1, chips):
-                    rx_copy(t, d, c).wait_recv()
-                    joined = joined + final[t, d, :, columns].astype(F32)
-                hidden_ref[t, :, columns] = joined.astype(BF16)
-                if sections > 1:
-                    z_copy(t, c).start()
-
         @pl.loop(0, micro)
         def _(t):
             if micro >= 3:
 
-                @pl.when(t == micro - 1)
+                @pl.when(t == 2)
                 def _():
                     finish(0)
 
@@ -371,30 +391,38 @@
                     for d in range(1, chips):
                         ax_copy(micro - 1, d, q).start()
 
-        @pl.loop(1 if micro >= 3 else 0, micro)
+        @pl.loop(2 if micro >= 3 else 0, micro)
         def _(t):
             finish(t)
 
-        for t in range(micro):
-            for d in range(1, chips):
-                ax_copy(t, d, q).wait_send()
-                for c in range(HOP_CUTS):
-                    rx_copy(t, d, c).wait_send()
-            for d in range(chips):
-                ad_copy(t, d, source(d, core)).wait_send()
-                rd_copy(t, d).wait_send()
+        for d in range(1, chips):
+            sent(gathered.at[:, q], ax_send.at[d - 1])
+            sent(incoming.at[:, d], rx_send.at[d - 1])
+        sent(outgoing, ad_send.at[0])
+        sent(outgoing, rd_send.at[0])
 
     def later_section():
         tiles = group // 2
-        plan = [(kind, k, d) for kind in range(2) for k in range(cuts[kind]) for d in range(1, chips)]
         for k in range(QUERY_CUTS):
             query_load(0, k).wait()
             for d in range(1, chips):
                 x_copy(0, d, k, q).start()
         transpose_out()
-        for k in range(cuts[1]):
+        rounds = [(kind, k) for kind in range(3) for k in range(cuts[kind])]
+        outs = rounds[cuts[0]:]
+
+        def send_out(one):
             for d in range(1, chips):
-                x_copy(1, d, k, q).start()
+                x_copy(one[0], d, one[1], q).start()
+
+        for one in outs[:AHEAD]:
+            send_out(one)
+
+        @pl.when(sec > 1)
+        def _():
+            for one in outs[AHEAD:]:
+                send_out(one)
+
         for j in range(1, groups):
             for k in range(QUERY_CUTS):
                 query_load(j, k).wait()
@@ -410,39 +438,56 @@
         for h in range(kv_heads):
             for b in range(2):
                 sink_rows[2 * h + b:2 * h + b + 1, :] = sink_row(h * group + b, tiles)
-        gain_load.wait()
         pair_load.wait()
 
-        def relay_y(kind, k, d):
-            for e in range(1, groups):
-                y_copy(kind, d, k, e, source(d, core), (g - e + groups) % groups).wait_recv()
-                d_copy(kind, d, k, e, source(d, core)).start()
-
-        previous = None
-        for kind, k, d in plan:
-            x_copy(kind, d, k, source(d, core)).wait_recv()
-            for e in range(1, groups):
-                y_copy(kind, d, k, e, source(d, core), g).start()
-            d_copy(kind, d, k, 0, source(d, core)).start()
-            if previous is not None:
-                relay_y(*previous)
-            previous = (kind, k, d)
-        if previous is not None:
-            relay_y(*previous)
-        for kind in range(2):
-            own_copy(kind, partner).wait_recv()
-        for kind, k, d in plan:
-            for e in range(groups):
-                d_copy(kind, d, k, e, source(d, 1 - core)).wait_recv()
+        def forward(kind, k):
+            for d in range(1, chips):
+                x_copy(kind, d, k, source(d, core)).wait_recv()
+                if kind < 2:
+                    for e in range(1, groups):
+                        y_copy(kind, d, k, e, source(d, core), g).start()
+                d_copy(kind, d, k, 0, source(d, core)).start()
+
+        def relay(kind, k):
+            if kind < 2:
+                for d in range(1, chips):
+                    for e in range(1, groups):
+                        y_copy(kind, d, k, e, source(d, core), (g - e + groups) % groups).wait_recv()
+                        d_copy(kind, d, k, e, source(d, core)).start()
+
+        def several(first, size):
+            return out_w.at[pl.ds(0, (chips - 1) * shard), pl.ds(first, size)]
+
+        def ready_queries():
+            own_copy(0, partner).wait_recv()
+            if chips > 1:
+                landed(query_w.at[pl.ds(0, chips - 1)], d_recv.at[0])
+
+        def ready(k):
+            if k == 0:
+                own_copy(1, partner).wait_recv()
+            if chips > 1:
+                landed(several(*out_edges[k]), d_recv.at[1 + k])
+
+        def gather_sent():
+            for kind in range(3):
+                for d in range(1, chips):
+                    sent(part_of(kind, q, g), x_send.at[kind, d - 1])
+                    for e in range(1, groups if kind < 2 else 1):
+                        sent(part_of(kind, source(d, core), g), y_send.at[kind, d - 1, e - 1])
+            if chips > 1:
+                sent(query_w.at[pl.ds(0, chips - 1)], d_send.at[0])
+                sent(several(0, last_edge[0]), d_send.at[1])
+                sent(several(*last_edge), d_send.at[2])
+            for kind in range(2):
+                own_copy(kind, q).wait_send()
 
         def enter(t):
-            for c in range(HOP_CUTS):
-                z_copy(t, c).wait_recv()
+            landed(arrive.at[t], z_recv.at[t])
             normed_ref[t] = norm(arrive[t])
             cache_of(t, normed_ref[t], cos_tab[mine], sin_tab[mine], True)
 
-        def attend(t):
-            length = length_ref[order_ref[t]]
+        def ask(t):
             normed = normed_ref[t]
             cosine, sine = cos_tab[mine], sin_tab[mine]
             for s in range(seq):
@@ -450,12 +495,14 @@
                 for p in range(shard // LANES):
                     rotated = rotate(queries[:, p * LANES:(p + 1) * LANES], cosine, sine) * 0.125
                     qbuf[:, s * shard + p * LANES:s * shard + (p + 1) * LANES] = rotated.astype(BF16)
+
+        def attend(t):
+            length = whole_ref[micro + whole_ref[t]]
             for off in range(1, depth + 1):
 
                 @pl.when(q >= off)
                 def _():
-                    w_copy(t, off, 0).wait_recv()
-                    w_copy(t, off, 1).wait_recv()
+                    landed(window.at[t, off - 1], w_recv.at[t, off - 1])
 
             bias = bias_of(q, length, tiles * rows)
 
@@ -476,40 +523,103 @@
                         [sink_rows[2 * h + b:2 * h + b + 1, :] for b in range(2)],
                     )
                     for p in range(tiles):
-                        cbuf[:, at[p]:at[p] + LANES] = some[p * rows:(p + 1) * rows]
-
-        def slot(t, carry):
+                        cbuf[t, :, at[p]:at[p] + LANES] = some[p * rows:(p + 1) * rows]
+
+        def leave(t, c, send=True):
+            first, size = edges[c]
+            columns = slice(first, first + size)
+            output = jnp.dot(cbuf[t], out_w[:, columns], preferred_element_type=F32)
+            hidden_ref[t, :, columns] = (arrive[t, :, columns].astype(F32) + output).astype(BF16)
+            if send:
+                z_copy(t, c).start()
+
+        needed = [[] for c in range(HOP_CUTS)]
+        for k, (first, size) in enumerate(out_edges):
+            needed[first // step].append(k)
+
+        @pl.when(sec == 1)
+        def _():
+            waiting, relayed = list(rounds), []
+
+            def forward_next():
+                if waiting:
+                    one = waiting.pop(0)
+                    forward(*one)
+                    at = rounds.index(one) + AHEAD
+                    if one[0] and at < len(rounds):
+                        send_out(rounds[at])
+                    relayed.append(one)
+
+            def relay_next():
+                if relayed:
+                    relay(*relayed.pop(0))
+
+            while len(waiting) > len(outs) - 2:
+                forward_next()
+                if len(relayed) > 1:
+                    relay_next()
+            while relayed and relayed[0][0] == 0:
+                relay_next()
+            ready_queries()
+            for what in SECOND_ORDER.split():
+                if what[0] == "f":
+                    forward_next()
+                elif what[0] == "r":
+                    relay_next()
+                elif what[0] == "w":
+                    for k in needed[int(what[1])]:
+                        ready(k)
+                elif what[0] == "o":
+                    leave(int(what[1]), int(what[2]), False)
+
+                    @pl.when(sec + 1 < sections)
+                    def _():
+                        z_copy(int(what[1]), int(what[2])).start()
+
+                else:
+                    (enter, ask, attend)["eqa".index(what[0])](int(what[1]))
+
+        @pl.when(sec > 1)
+        def _():
+            previous = None
+            for one in rounds:
+                forward(*one)
+                if previous is not None:
+                    relay(*previous)
+                previous = one
+            relay(*previous)
+            ready_queries()
+            for k in range(len(out_edges)):
+                ready(k)
+            gather_sent()
+
+        def slot(send, t, carry):
             enter(t)
+            ask(t)
             attend(t)
-            for c, (first, size) in enumerate(edges):
-                columns = slice(first, first + size)
-                output = jnp.dot(cbuf[...], out_w[:, columns], preferred_element_type=F32)
-                hidden_ref[t, :, columns] = (arrive[t, :, columns].astype(F32) + output).astype(BF16)
-
-                @pl.when(sec + 1 < sections)
-                def _():
-                    z_copy(t, c).start()
-
+            for c in range(HOP_CUTS):
+                leave(t, c, send)
             return carry
 
-        lax.fori_loop(0, micro, slot, 0)
-
-        for kind, k, d in plan:
-            x_copy(kind, d, k, q).wait_send()
-            for e in range(1, groups):
-                y_copy(kind, d, k, e, source(d, core), g).wait_send()
-            for e in range(groups):
-                d_copy(kind, d, k, e, source(d, core)).wait_send()
-        for kind in range(2):
-            own_copy(kind, q).wait_send()
-        for t in range(micro):
-            for off in range(1, depth + 1):
-
-                @pl.when(q + off < seq)
-                def _():
-                    w_copy(t, off, 0).wait_send()
-                    w_copy(t, off, 1).wait_send()
-
+        start = jnp.where(sec == 1, 2, 0)
+
+        @pl.when(sec + 1 < sections)
+        def _():
+            lax.fori_loop(start, micro, functools.partial(slot, True), 0)
+
+        @pl.when(sec + 1 == sections)
+        def _():
+            lax.fori_loop(start, micro, functools.partial(slot, False), 0)
+
+        @pl.when(sec == 1)
+        def _():
+            gather_sent()
+
+        for off in range(1, depth + 1):
+
+            @pl.when(q + off < seq)
+            def _():
+                sent(window.at[:, off - 1], w_send.at[off - 1])
 
     @pl.when(sec == 0)
     def _():
@@ -521,9 +631,7 @@
 
     @pl.when(sec + 1 < sections)
     def _():
-        for t in range(micro):
-            for c in range(HOP_CUTS):
-                z_copy(t, c).wait_send()
+        sent(arrive, z_send.at[0])
 
 
 def per_device(
@@ -539,8 +647,10 @@
     chips = seq // 2
     keep = min(WIN, rows)
     depth = WIN // keep
-    most = max(QUERY_CUTS, -(-width // OUT_STEP))
-    limit = (52 if seq * rows <= 512 else 57) * 1024 * 1024
+    others, peers = max(1, chips - 1), max(1, groups - 1)
+    rounds = QUERY_CUTS + len(out_pieces(width))
+    limit = 55488512 if seq * rows <= 512 else 57 * 1024 * 1024
+    real = jnp.concatenate([norm_gain, sink_logits], 1)
     dma = pltpu.SemaphoreType.DMA
     vmem = pl.BlockSpec(memory_space=pltpu.VMEM)
     smem = pl.BlockSpec(memory_space=pltpu.SMEM)
@@ -551,11 +661,10 @@
             jax.ShapeDtypeStruct((micro, rows, width), BF16),
             jax.ShapeDtypeStruct((micro, rows, pair_width), BF16),
         ),
-        in_specs=[smem] * 3 + [hbm] * 5,
+        in_specs=[smem, smem, vmem] + [hbm] * 4,
         out_specs=(vmem, vmem),
         scratch_shapes=[
             pltpu.VMEM((micro, rows, width), BF16),
-            pltpu.VMEM((1, width), F32),
             pltpu.VMEM((width, pair_width), BF16),
             pltpu.VMEM((width, shard), BF16),
             pltpu.VMEM((seq * rows, LANES), F32),
@@ -567,7 +676,7 @@
             pltpu.VMEM((micro, rows, width), BF16),
             pltpu.VMEM((micro, rows, width), BF16),
             pltpu.VMEM((rows, seq * shard), BF16),
-            pltpu.VMEM((rows, seq * shard), BF16),
+            pltpu.VMEM((micro, rows, seq * shard), BF16),
             pltpu.VMEM((2 * kv_heads, lanes), F32),
             pltpu.VMEM((micro, seq, rows, width), BF16),
             pltpu.VMEM((seq * rows, shard), BF16),
@@ -578,34 +687,34 @@
             pltpu.VMEM((micro, chips, rows, width), BF16),
             pltpu.VMEM((micro, chips, rows, width), BF16),
             pltpu.VMEM((micro, rows, width), F32),
-            dma((groups * QUERY_CUTS + 4,)),
-            dma((2, chips, most)),
-            dma((2, chips, most)),
-            dma((2, chips, most, groups)),
-            dma((2, chips, most, groups)),
-            dma((2, chips, most, groups)),
-            dma((2, chips, most, groups)),
+            dma((groups * QUERY_CUTS + 3,)),
+            dma((3, others)),
+            dma((others, rounds)),
+            dma((3, others, peers)),
+            dma((others, rounds, peers)),
+            dma((3,)),
+            dma((rounds,)),
             dma((2,)),
             dma((2,)),
-            dma((micro, depth, 2)),
-            dma((micro, depth, 2)),
-            dma((micro, HOP_CUTS)),
-            dma((micro, HOP_CUTS)),
+            dma((depth,)),
+            dma((micro, depth)),
+            dma((1,)),
+            dma((micro,)),
+            dma((others,)),
+            dma((micro, others)),
+            dma((1,)),
+            dma((micro,)),
+            dma((1,)),
             dma((micro, chips)),
-            dma((micro, chips)),
-            dma((micro, chips)),
-            dma((micro, chips)),
-            dma((micro, chips)),
-            dma((micro, chips)),
-            dma((micro, chips, HOP_CUTS)),
-            dma((micro, chips, HOP_CUTS)),
+            dma((others,)),
+            dma((micro, others, HOP_CUTS)),
         ],
         compiler_params=pltpu.CompilerParams(
             collective_id=0, has_side_effects=True, vmem_limit_bytes=limit
         ),
     )(
-        block_order, prompt_lengths, sink_logits[0],
-        tokens, norm_gain, w_key_value[0], w_query[0], w_out[0].T,
+        jnp.concatenate([block_order, prompt_lengths]), real, real,
+        tokens, w_key_value[0], w_query[0], w_out[0].T,
     )
     return hidden[None], cache[None]
 

time: 92.2 us -> 80.2 us (0.87)
  Pallas kernels: 86 us -> 75.6 us
  local copies, waits for them, and re-layouts: 5.37 us -> 1.58 us
  other arithmetic: 0 us -> 1.53 us
    pallas_call x1, Pallas kernels: 86 us -> 75.6 us  [per_device(): pl.pallas_call(functools.partial(kernel, shape), out_shape=(jax.ShapeDtyp...]
    unnamed x12 -> x2, local copies, waits for them, and re-layouts: 5.37 us -> 1.58 us
    concatenate x0 -> x2, other arithmetic: none -> 1.53 us  [the longest x1 0.78 us: per_device(): real = jnp.concatenate([norm_gain, sink_logits], 1)]
where the time goes in v2:
time: 80.2 us; the launch traced here: 79.3 us
  Pallas kernels  75.6 us (94%)
  local copies, waits for them, and re-layouts  1.58 us (2%)
  other arithmetic  1.53 us (2%)
    pallas_call x1, Pallas kernels, per_device(): pl.pallas_call(functools.partial(kernel, shape), out_shape=(jax.ShapeDtyp...  75.6 us

profile of v2, /device:TPU:27, one launch (start us, length us, event | category | flops | bytes accessed | tf_op | source)
XLA Modules:
  0.0 79.3 jit_solution(5453362399983082473)
XLA Ops:
  0.6 0.7 pad_add_fusion.whole_ref
  1.4 0.8 pad_maximum_fusion.real_ref.real_row
  2.2 75.6 %shard_map.95 = (bf16[4,64,1440]{2,1,0:T(8,128)(2,1)S(1)}, bf16[4,64,512]{2,1,0:T(8,128)(2,1)S(1)}) custom-call(s32[8]{0:T(128)S(1)} %pad_add_fusion.whole_ref, f32[1,1472]{1,0:T(1,128)S(1)} %pad_maximum_fusion.real_ref.real_row, f32[1,1472]{1,0:T(1,128)S(1)} %pad_maximum_fusion.real_ref.real_row, bf16[4,64,1440]{2,1,0:T(8,128)(2,1)} %tokens_hbm.1, ...), custom_call_target="tpu_custom_call" | custom-call | tf_op jit(solution)/shard_map/pallas_call | solution.py:658
  77.8 0.9 %copy.12 = bf16[1,4,64,1440]{3,2,1,0:T(8,128)(2,1)} copy(bf16[1,4,64,1440]{3,2,1,0:T(8,128)(2,1)S(1)} %bitcast.7) | data formatting | bytes 1474560
  78.6 0.7 copy.13

commit v3 on v2

--- a/solution.py
+++ b/solution.py
@@ -19,8 +19,18 @@
 QUERY_CUTS = 5
 OUT_STEP = 256
 HOP_CUTS = 3
-SECOND_ORDER = "e0 f q0 r f r f f a0 w0 o00 r e1 r q1 w1 o01 r f w2 o02 a1 o10 o11 o12"
-AHEAD = 2
+SECOND_ORDER = (
+    "e0", "f", "q0", "r", "f", "r", "f", "f", "a0", "w0", "o00", "r",
+    "e1", "r", "q1", "w1", "o01", "r", "f", "w2", "o02", "a1", "o10", "o11", "o12",
+)
+AHEAD = 3
+
+
+def query_pieces(length):
+    size = length // QUERY_CUTS
+    small = size // 3
+    edges = [(0, small), (small, size - small)]
+    return edges + [(k * size, size) for k in range(1, QUERY_CUTS)]
 
 
 def out_pieces(width):
@@ -33,7 +43,7 @@
 
 def kernel(
     shape,
-    whole_ref, real_ref, real_row,
+    small_ref, small_row,
     tokens_hbm, pair_hbm, query_hbm, out_hbm,
     hidden_ref, cache_ref,
     tokens_ref, pair_ref, out_t, cos_tab, sin_tab,
@@ -63,20 +73,22 @@
     half = HEAD_DIM // 2
     own_heads = shard // HEAD_DIM
 
-    query_size = width // groups // QUERY_CUTS
+    query_rows = width // groups
+    query_edges = query_pieces(query_rows)
     out_rows = shard // groups
     out_edges = out_pieces(width)
     last_edge = out_edges[-1]
-    cuts = (QUERY_CUTS, len(out_edges) - 1, 1)
+    cuts = (len(query_edges), len(out_edges) - 1, 1)
 
     def query_load(j, k):
-        first = pl.multiple_of((((g + j) % groups) * QUERY_CUTS + k) * query_size, 16)
+        first = pl.multiple_of(((g + j) % groups) * query_rows + query_edges[k][0], 16)
+        size = query_edges[k][1]
         return pltpu.make_async_copy(
-            query_hbm.at[pl.ds(first, query_size)], query_w.at[q, pl.ds(first, query_size)],
-            local_sem.at[j * QUERY_CUTS + k],
-        )
-
-    base = groups * QUERY_CUTS
+            query_hbm.at[pl.ds(first, size)], query_w.at[q, pl.ds(first, size)],
+            local_sem.at[j * cuts[0] + k],
+        )
+
+    base = groups * cuts[0]
     out_load = pltpu.make_async_copy(out_hbm, out_t, local_sem.at[base])
     pair_load = pltpu.make_async_copy(pair_hbm, pair_ref, local_sem.at[base + 1])
     tokens_load = pltpu.make_async_copy(tokens_hbm, tokens_ref, local_sem.at[base + 2])
@@ -86,7 +98,7 @@
         tokens_load.start()
 
     for j in range(groups):
-        for k in range(QUERY_CUTS):
+        for k in range(cuts[0]):
             query_load(j, k).start()
     out_load.start()
     pair_load.start()
@@ -121,8 +133,8 @@
 
     def piece(kind, owner, part, k):
         if kind == 0:
-            first = (part * QUERY_CUTS + k) * query_size
-            return query_w.at[owner, pl.ds(pl.multiple_of(first, 16), query_size)]
+            first = part * query_rows + query_edges[k][0]
+            return query_w.at[owner, pl.ds(pl.multiple_of(first, 16), query_edges[k][1])]
         if kind == 2:
             return out_w.at[own_rows(owner), pl.ds(*last_edge)]
         first = pl.multiple_of(owner * shard + part * out_rows, out_rows)
@@ -151,8 +163,7 @@
 
     def part_of(kind, owner, part):
         if kind == 0:
-            size = QUERY_CUTS * query_size
-            return query_w.at[owner, pl.ds(pl.multiple_of(part * size, 16), size)]
+            return query_w.at[owner, pl.ds(pl.multiple_of(part * query_rows, 16), query_rows)]
         if kind == 2:
             return piece(2, owner, part, 0)
         first = pl.multiple_of(owner * shard + part * out_rows, out_rows)
@@ -203,6 +214,17 @@
             incoming.at[t, d, :, columns], final.at[t, d, :, columns],
             rx_send.at[d - 1], rx_recv.at[t, d - 1, c], {"seq": ahead(d, core)},
         )
+
+    after = width + heads_width // HEAD_DIM
+
+    def order_of(t):
+        return small_ref[0, after + t]
+
+    def length_of(t):
+        length = small_ref[0, after + micro]
+        for b in range(1, micro):
+            length = jnp.where(order_of(t) == b, small_ref[0, after + micro + b], length)
+        return length
 
     def tables(r):
         lane = lax.broadcasted_iota(jnp.int32, (rows, LANES), 1)
@@ -225,7 +247,7 @@
     def norm(h):
         widened = h.astype(F32)
         scale = lax.rsqrt(jnp.mean(widened * widened, -1, keepdims=True) + EPSILON)
-        return (widened * scale * real_row[:, :width]).astype(BF16)
+        return (widened * scale * small_row[:, :width]).astype(BF16)
 
     def transpose_out():
         out_load.wait()
@@ -238,33 +260,39 @@
         row = lax.broadcasted_iota(jnp.int32, (span, lanes), 1) % rows
         column = key + r * rows
         allowed = (key <= row) & (row - key < WIN) & (column >= 0)
-        allowed = allowed & ((column < length) | (key == row))
+        allowed = allowed & ((column.astype(F32) < length) | (key == row))
         return jnp.where(allowed, F32(0.0), F32(-1e30))
 
     def sink_row(first, tiles):
         return jnp.concatenate(
-            [jnp.full((1, rows), real_ref[0, width + first + 2 * p], F32) for p in range(tiles)], 1
+            [jnp.full((1, rows), small_ref[0, width + first + 2 * p], F32) for p in range(tiles)], 1
         )
 
     low = lax.broadcasted_iota(jnp.int32, (span, LANES), 1) < HEAD_DIM
     ones = jnp.ones((16, span), BF16)
 
-    def attention(pairs, twice, values_t, bias, sinks):
-        zero = jnp.zeros_like(twice)
-        sides = jnp.concatenate([jnp.where(low, twice, zero), jnp.where(low, zero, twice)], 0)
-        scores = lax.dot_general(
-            sides, jnp.concatenate(pairs, 0), (((1,), (1,)), ((), ())), preferred_element_type=F32
-        )
-        extended = jnp.concatenate([values_t, ones], 0)
-        parts = []
-        for b in range(2):
-            masked = scores[b * span:(b + 1) * span] + bias
-            top = jnp.maximum(jnp.max(masked, 0, keepdims=True), sinks[b])
-            expo = jnp.exp(masked - top).astype(BF16)
-            summed = jnp.dot(extended, expo, preferred_element_type=F32)
-            whole_sum = summed[HEAD_DIM:HEAD_DIM + 1] + jnp.exp(sinks[b] - top)
-            parts.append(summed[:HEAD_DIM] * (1.0 / whole_sum))
-        return jnp.concatenate(parts, 0).T.astype(BF16)
+    def attention(jobs):
+        scores = []
+        for pairs, twice, _, _, _ in jobs:
+            zero = jnp.zeros_like(twice)
+            sides = jnp.concatenate([jnp.where(low, twice, zero), jnp.where(low, zero, twice)], 0)
+            scores.append(lax.dot_general(
+                sides, jnp.concatenate(pairs, 0), (((1,), (1,)), ((), ())),
+                preferred_element_type=F32,
+            ))
+        results = []
+        for (_, _, values_t, bias, sinks), score in zip(jobs, scores):
+            extended = jnp.concatenate([values_t, ones], 0)
+            parts = []
+            for b in range(2):
+                masked = score[b * span:(b + 1) * span] + bias
+                top = jnp.maximum(jnp.max(masked, 0, keepdims=True), sinks[b])
+                expo = jnp.exp(masked - top).astype(BF16)
+                summed = jnp.dot(extended, expo, preferred_element_type=F32)
+                whole_sum = summed[HEAD_DIM:HEAD_DIM + 1] + jnp.exp(sinks[b] - top)
+                parts.append(summed[:HEAD_DIM] * (1.0 / whole_sum))
+            results.append(jnp.concatenate(parts, 0).T.astype(BF16))
+        return results
 
     def cache_of(t, normed, cosine, sine, send):
         keys = jnp.dot(normed, pair_ref[:, :kv_width], preferred_element_type=F32)
@@ -286,7 +314,10 @@
         tiles = shard // LANES
         tokens_load.wait()
         for t in range(micro):
-            hbuf[t] = tokens_ref[whole_ref[t]]
+            block = tokens_ref[0]
+            for b in range(1, micro):
+                block = jnp.where(order_of(t) == b, tokens_ref[b], block)
+            hbuf[t] = block
             gathered[t, q] = norm(hbuf[t])
             if t < micro - 1 or micro < 3:
                 for d in range(1, chips):
@@ -299,7 +330,7 @@
         transpose_out()
         pair_load.wait()
         for j in range(groups):
-            for k in range(QUERY_CUTS):
+            for k in range(cuts[0]):
                 query_load(j, k).wait()
         for t in range(micro):
             cache_of(t, gathered[t, q], cos_tab[mine], sin_tab[mine], False)
@@ -331,7 +362,7 @@
                 ax_copy(t, d, source(d, core)).wait_recv()
                 ad_copy(t, d, source(d, core)).start()
             landed(outgoing.at[t], ad_recv.at[t])
-            length = whole_ref[micro + whole_ref[t]]
+            length = length_of(t)
             normed = gathered[t].reshape(total, width)
             cosine, sine = cos_tab[...], sin_tab[...]
             keys = jnp.dot(normed, pair_ref[:, pair_at], preferred_element_type=F32)
@@ -341,14 +372,17 @@
             for p in range(tiles):
                 tile = slice(p * LANES, (p + 1) * LANES)
                 tq[:, tile] = (rotate(queries[:, tile], cosine, sine) * 0.125).astype(BF16)
+            jobs = []
             for r in range(seq):
                 at = slice(r * rows, r * rows + span)
-                some = attention(
+                jobs.append((
                     [tq[r * rows:(r + 1) * rows, p * LANES:(p + 1) * LANES] for p in range(tiles)],
                     kd_buf[at], vd_buf[at].T[:HEAD_DIM], bias_of(r, length, tiles * rows), sinks,
-                )
+                ))
+            for r, some in enumerate(attention(jobs)):
                 for p in range(tiles):
                     ctx[r, :, p * LANES:(p + 1) * LANES] = some[p * rows:(p + 1) * rows]
+
             if micro >= 3:
 
                 @pl.when(t == micro - 1)
@@ -403,7 +437,7 @@
 
     def later_section():
         tiles = group // 2
-        for k in range(QUERY_CUTS):
+        for k in range(cuts[0]):
             query_load(0, k).wait()
             for d in range(1, chips):
                 x_copy(0, d, k, q).start()
@@ -424,7 +458,7 @@
                 send_out(one)
 
         for j in range(1, groups):
-            for k in range(QUERY_CUTS):
+            for k in range(cuts[0]):
                 query_load(j, k).wait()
         for kind in range(2):
             own_copy(kind, q).start()
@@ -497,7 +531,7 @@
                     qbuf[:, s * shard + p * LANES:s * shard + (p + 1) * LANES] = rotated.astype(BF16)
 
         def attend(t):
-            length = whole_ref[micro + whole_ref[t]]
+            length = length_of(t)
             for off in range(1, depth + 1):
 
                 @pl.when(q >= off)
@@ -511,19 +545,22 @@
                 parts = [window[t, off - 1, :, at] for off in range(depth, 0, -1)]
                 return jnp.concatenate(parts + [cache_ref[t, :, at]], 0)
 
+            jobs = []
             for pair in range(kv_heads // 2):
                 values_t = span_of(kv_width + pair * LANES, LANES).T
                 for e in range(2):
                     h = pair * 2 + e
                     head = span_of(h * HEAD_DIM, HEAD_DIM)
-                    at = [(h * tiles + p) * LANES for p in range(tiles)]
-                    some = attention(
-                        [qbuf[:, a:a + LANES] for a in at], jnp.concatenate([head, head], 1),
+                    jobs.append((
+                        [qbuf[:, a:a + LANES] for a in range(h * tiles * LANES, (h + 1) * tiles * LANES, LANES)],
+                        jnp.concatenate([head, head], 1),
                         values_t[e * HEAD_DIM:(e + 1) * HEAD_DIM], bias,
                         [sink_rows[2 * h + b:2 * h + b + 1, :] for b in range(2)],
-                    )
-                    for p in range(tiles):
-                        cbuf[t, :, at[p]:at[p] + LANES] = some[p * rows:(p + 1) * rows]
+                    ))
+            for h, some in enumerate(attention(jobs)):
+                for p in range(tiles):
+                    at = (h * tiles + p) * LANES
+                    cbuf[t, :, at:at + LANES] = some[p * rows:(p + 1) * rows]
 
         def leave(t, c, send=True):
             first, size = edges[c]
@@ -561,7 +598,7 @@
             while relayed and relayed[0][0] == 0:
                 relay_next()
             ready_queries()
-            for what in SECOND_ORDER.split():
+            for what in SECOND_ORDER:
                 if what[0] == "f":
                     forward_next()
                 elif what[0] == "r":
@@ -648,9 +685,16 @@
     keep = min(WIN, rows)
     depth = WIN // keep
     others, peers = max(1, chips - 1), max(1, groups - 1)
-    rounds = QUERY_CUTS + len(out_pieces(width))
+    queries = len(query_pieces(width // groups))
+    rounds = queries + len(out_pieces(width))
     limit = 55488512 if seq * rows <= 512 else 57 * 1024 * 1024
-    real = jnp.concatenate([norm_gain, sink_logits], 1)
+    parts = [norm_gain, sink_logits, block_order[None].astype(F32), prompt_lengths[None].astype(F32)]
+    small_width = sum(part.shape[1] for part in parts)
+    small, first = 0.0, 0
+    for part in parts:
+        behind = small_width - first - part.shape[1]
+        small = small + jnp.pad(part, ((0, 0), (first, behind)))
+        first += part.shape[1]
     dma = pltpu.SemaphoreType.DMA
     vmem = pl.BlockSpec(memory_space=pltpu.VMEM)
     smem = pl.BlockSpec(memory_space=pltpu.SMEM)
@@ -661,7 +705,7 @@
             jax.ShapeDtypeStruct((micro, rows, width), BF16),
             jax.ShapeDtypeStruct((micro, rows, pair_width), BF16),
         ),
-        in_specs=[smem, smem, vmem] + [hbm] * 4,
+        in_specs=[smem, vmem] + [hbm] * 4,
         out_specs=(vmem, vmem),
         scratch_shapes=[
             pltpu.VMEM((micro, rows, width), BF16),
@@ -687,7 +731,7 @@
             pltpu.VMEM((micro, chips, rows, width), BF16),
             pltpu.VMEM((micro, chips, rows, width), BF16),
             pltpu.VMEM((micro, rows, width), F32),
-            dma((groups * QUERY_CUTS + 3,)),
+            dma((groups * queries + 3,)),
             dma((3, others)),
             dma((others, rounds)),
             dma((3, others, peers)),
@@ -713,7 +757,7 @@
             collective_id=0, has_side_effects=True, vmem_limit_bytes=limit
         ),
     )(
-        jnp.concatenate([block_order, prompt_lengths]), real, real,
+        small, small,
         tokens, w_key_value[0], w_query[0], w_out[0].T,
     )
     return hidden[None], cache[None]

time: 80.2 us -> 78.2 us (0.975)
  Pallas kernels: 75.6 us -> 74.3 us
    concatenate x2 -> x0, other arithmetic: 1.53 us -> none  [the longest x1 0.78 us: per_device(): real = jnp.concatenate([norm_gain, sink_logits], 1)]
    pallas_call x1, Pallas kernels: 75.6 us -> 74.3 us  [per_device(): pl.pallas_call(functools.partial(kernel, shape), out_shape=(jax.ShapeDtyp...]
where the time goes in v3:
time: 78.2 us; the launch traced here: 78 us
  Pallas kernels  74.3 us (95%)
  local copies, waits for them, and re-layouts  1.58 us (2%)
  other arithmetic  1.46 us (2%)
    pallas_call x1, Pallas kernels, per_device(): pl.pallas_call(functools.partial(kernel, shape), out_shape=(jax.ShapeDtyp...  74.3 us
    unnamed x2, local copies, waits for them, and re-layouts  1.58 us

profile of v3, /device:TPU:27, one launch (start us, length us, event | category | flops | bytes accessed | tf_op | source)
XLA Modules:
  0.0 78.0 jit_solution(2825739776452534845)
XLA Ops:
  0.6 0.7 convert_bitcast_fusion
  1.3 0.8 %pad_add_fusion.small_ref.small_row = f32[1,1480]{1,0:T(1,128)S(1)} fusion(f32[1,4]{1,0:T(1,128)S(1)} %get-tuple-element.6, f32[1,4]{1,0:T(1,128)S(1)} %get-tuple-element.7, f32[1,32]{1,0:T(1,128)} %param.15, f32[1,1440]{1,0:T(1,128)} %param.11), kind=kLoop, calls=%fused_computation | loop fusion | flops 4440 | bytes 11840 | tf_op jit(solution)/shard_map/add | solution.py:696
  2.1 74.3 %shard_map.95 = (bf16[4,64,1440]{2,1,0:T(8,128)(2,1)S(1)}, bf16[4,64,512]{2,1,0:T(8,128)(2,1)S(1)}) custom-call(f32[1,1480]{1,0:T(1,128)S(1)} %pad_add_fusion.small_ref.small_row, f32[1,1480]{1,0:T(1,128)S(1)} %pad_add_fusion.small_ref.small_row, bf16[4,64,1440]{2,1,0:T(8,128)(2,1)} %tokens_hbm.1, bf16[1440,512]{1,0:T(8,128)(2,1)} %bitcast.13, ...), custom_call_target="tpu_custom_call" | custom-call | tf_op jit(solution)/shard_map/pallas_call | solution.py:702
  76.4 0.9 %copy.12 = bf16[1,4,64,1440]{3,2,1,0:T(8,128)(2,1)} copy(bf16[1,4,64,1440]{3,2,1,0:T(8,128)(2,1)S(1)} %bitcast.11) | data formatting | bytes 1474560
  77.3 0.7 copy.13

commit v4 on v3

--- a/solution.py
+++ b/solution.py
@@ -562,13 +562,13 @@
                     at = (h * tiles + p) * LANES
                     cbuf[t, :, at:at + LANES] = some[p * rows:(p + 1) * rows]
 
-        def leave(t, c, send=True):
-            first, size = edges[c]
+        def leave(t, edge, send):
+            first, size = edge
             columns = slice(first, first + size)
             output = jnp.dot(cbuf[t], out_w[:, columns], preferred_element_type=F32)
             hidden_ref[t, :, columns] = (arrive[t, :, columns].astype(F32) + output).astype(BF16)
             if send:
-                z_copy(t, c).start()
+                z_copy(t, edges.index(edge)).start()
 
         needed = [[] for c in range(HOP_CUTS)]
         for k, (first, size) in enumerate(out_edges):
@@ -607,7 +607,7 @@
                     for k in needed[int(what[1])]:
                         ready(k)
                 elif what[0] == "o":
-                    leave(int(what[1]), int(what[2]), False)
+                    leave(int(what[1]), edges[int(what[2])], False)
 
                     @pl.when(sec + 1 < sections)
                     def _():
@@ -634,8 +634,8 @@
             enter(t)
             ask(t)
             attend(t)
-            for c in range(HOP_CUTS):
-                leave(t, c, send)
+            for edge in edges if send else [(0, width)]:
+                leave(t, edge, send)
             return carry
 
         start = jnp.where(sec == 1, 2, 0)
@@ -688,13 +688,12 @@
     queries = len(query_pieces(width // groups))
     rounds = queries + len(out_pieces(width))
     limit = 55488512 if seq * rows <= 512 else 57 * 1024 * 1024
-    parts = [norm_gain, sink_logits, block_order[None].astype(F32), prompt_lengths[None].astype(F32)]
-    small_width = sum(part.shape[1] for part in parts)
-    small, first = 0.0, 0
-    for part in parts:
-        behind = small_width - first - part.shape[1]
-        small = small + jnp.pad(part, ((0, 0), (first, behind)))
-        first += part.shape[1]
+    heads = sink_logits.shape[1]
+    small = jnp.pad(norm_gain, ((0, 0), (0, heads + 2 * micro)))
+    small = small + jnp.pad(sink_logits, ((0, 0), (width, 2 * micro)))
+    places = jnp.pad(block_order[None], ((0, 0), (width + heads, micro)))
+    places = places + jnp.pad(prompt_lengths[None], ((0, 0), (width + heads + micro, 0)))
+    small = small + places.astype(F32)
     dma = pltpu.SemaphoreType.DMA
     vmem = pl.BlockSpec(memory_space=pltpu.VMEM)
     smem = pl.BlockSpec(memory_space=pltpu.SMEM)
@@ -737,7 +736,7 @@
             dma((3, others, peers)),
             dma((others, rounds, peers)),
             dma((3,)),
-            dma((rounds,)),
+            dma((1 + rounds - queries,)),
             dma((2,)),
             dma((2,)),
             dma((depth,)),

time: 78.2 us -> 77.5 us (level)
  no operation moved by 1% of the time
where the time goes in v4:
time: 77.5 us; the launch traced here: 77.3 us
  Pallas kernels  74.2 us (96%)
  local copies, waits for them, and re-layouts  1.58 us (2%)
  other arithmetic  0.82 us (1%)
    pallas_call x1, Pallas kernels, per_device(): pl.pallas_call(functools.partial(kernel, shape), out_shape=(jax.ShapeDtyp...  74.2 us
    unnamed x2, local copies, waits for them, and re-layouts  1.58 us

profile of v4, /device:TPU:27, one launch (start us, length us, event | category | flops | bytes accessed | tf_op | source)
XLA Modules:
  0.0 77.3 jit_solution(761079276109994281)
XLA Ops:
  0.6 0.8 %convert_add_fusion.small_ref.small_row = f32[1,1480]{1,0:T(1,128)S(1)} fusion(s32[1,4]{1,0:T(1,128)} %bitcast.14, s32[1,4]{1,0:T(1,128)} %bitcast.15, f32[1,32]{1,0:T(1,128)} %param.15, f32[1,1440]{1,0:T(1,128)} %param.11), kind=kLoop, calls=%fused_computation | loop fusion | flops 5920 | bytes 11840 | tf_op jit(solution)/shard_map/add | solution.py:696
  1.4 74.2 %shard_map.95 = (bf16[4,64,1440]{2,1,0:T(8,128)(2,1)S(1)}, bf16[4,64,512]{2,1,0:T(8,128)(2,1)S(1)}) custom-call(f32[1,1480]{1,0:T(1,128)S(1)} %convert_add_fusion.small_ref.small_row, f32[1,1480]{1,0:T(1,128)S(1)} %convert_add_fusion.small_ref.small_row, bf16[4,64,1440]{2,1,0:T(8,128)(2,1)} %tokens_hbm.1, bf16[1440,512]{1,0:T(8,128)(2,1)} %bitcast.11, ...), custom_call_target="tpu_custom_call" | custom-call | tf_op jit(solution)/shard_map/pallas_call | solution.py:701
  75.7 0.9 %copy.12 = bf16[1,4,64,1440]{3,2,1,0:T(8,128)(2,1)} copy(bf16[1,4,64,1440]{3,2,1,0:T(8,128)(2,1)S(1)} %bitcast.9) | data formatting | bytes 1474560
  76.6 0.7 copy.13

commit v5 on v4

--- a/solution.py
+++ b/solution.py
@@ -23,7 +23,7 @@
     "e0", "f", "q0", "r", "f", "r", "f", "f", "a0", "w0", "o00", "r",
     "e1", "r", "q1", "w1", "o01", "r", "f", "w2", "o02", "a1", "o10", "o11", "o12",
 )
-AHEAD = 3
+AHEAD = 4
 
 
 def query_pieces(length):

time: 77.5 us -> 77.5 us (level)
  no operation moved by 1% of the time
where the time goes in v5:
time: 77.5 us; the launch traced here: 77.3 us
  Pallas kernels  74.2 us (96%)
  local copies, waits for them, and re-layouts  1.58 us (2%)
  other arithmetic  0.82 us (1%)
    pallas_call x1, Pallas kernels, per_device(): pl.pallas_call(functools.partial(kernel, shape), out_shape=(jax.ShapeDtyp...  74.2 us
    unnamed x2, local copies, waits for them, and re-layouts  1.58 us

profile of v5, /device:TPU:27, one launch (start us, length us, event | category | flops | bytes accessed | tf_op | source)
XLA Modules:
  0.0 77.3 jit_solution(11509587935668954713)
XLA Ops:
  0.6 0.8 %convert_add_fusion.small_ref.small_row = f32[1,1480]{1,0:T(1,128)S(1)} fusion(s32[1,4]{1,0:T(1,128)} %bitcast.14, s32[1,4]{1,0:T(1,128)} %bitcast.15, f32[1,32]{1,0:T(1,128)} %param.15, f32[1,1440]{1,0:T(1,128)} %param.11), kind=kLoop, calls=%fused_computation | loop fusion | flops 5920 | bytes 11840 | tf_op jit(solution)/shard_map/add | solution.py:696
  1.4 74.2 %shard_map.95 = (bf16[4,64,1440]{2,1,0:T(8,128)(2,1)S(1)}, bf16[4,64,512]{2,1,0:T(8,128)(2,1)S(1)}) custom-call(f32[1,1480]{1,0:T(1,128)S(1)} %convert_add_fusion.small_ref.small_row, f32[1,1480]{1,0:T(1,128)S(1)} %convert_add_fusion.small_ref.small_row, bf16[4,64,1440]{2,1,0:T(8,128)(2,1)} %tokens_hbm.1, bf16[1440,512]{1,0:T(8,128)(2,1)} %bitcast.11, ...), custom_call_target="tpu_custom_call" | custom-call | tf_op jit(solution)/shard_map/pallas_call | solution.py:701
  75.7 0.9 %copy.12 = bf16[1,4,64,1440]{3,2,1,0:T(8,128)(2,1)} copy(bf16[1,4,64,1440]{3,2,1,0:T(8,128)(2,1)S(1)} %bitcast.9) | data formatting | bytes 1474560
  76.6 0.7 copy.13
